TPU v7x, 32 devices: a whole 2x2x4 slice. The times are simulated.
32 devices in a mesh: ctx: 16 (over z, y, core), tp: 2 (over x).
Axes of the slice: x: 2, y: 2, z: 4, core: 2. Of those that a mesh axis runs over, the one named last changes fastest.
Arguments:
- tokens: bfloat16 [4096, 8192], P(('ctx', 'tp')), may hold values from -64 to 64
- query_weight: bfloat16 [8192, 1024], P(None, 'tp'), may hold values from -0.0625 to 0.0625
- keyval_weight: bfloat16 [8192, 512], P(None, 'tp'), may hold values from -0.0625 to 0.0625
- doc_lengths: int32 [32], replicated, may hold values from 1 to 2048, 4096 in all
- owners: int32 [128], replicated, may hold values from 0 to 15, as said below
Outputs:
- attended: bfloat16 [4096, 1024], P('ctx', 'tp')
Inputs may be any that keep to these rules, and one draw needn't show every extreme that they name: The 8 blocks of one index of ctx (blocks i * 8 to (i + 1) * 8 - 1) go to 8 different owners; for each position j < 8, the blocks i * 8 + j of all indices i go to all different owners, so every owner receives exactly one block of each position.
All inputs are finite; a program needn't handle non-finite values.
Results may differ from a plain program's by a relative error of at most 0.0055.
The roundings to bfloat16 on the way count: a program that leaves them out, or rounds other values in their place, can miss the bound.
Values may be sent and summed in bfloat16 or wider, within the bound.
No kernel may reach another device: no remote copies, remote signals or barrier semaphores. Data moves between devices by JAX's collectives and lax.ppermute only.
A program may use at most 128 MiB of HBM per device.

v0:
```python
import functools
import math

import jax
import jax.numpy as jnp
from jax import lax
from jax.experimental import pallas as pl
from jax.experimental.pallas import tpu as pltpu
from jax.sharding import PartitionSpec as P


NEG_FILL = -1e30
LOG2E = 1.4426950408889634
UNROLL = 8


def route(queries, target_ref, send_ref):
    block_len = send_ref.shape[1]
    block = 0
    for query in queries:
        for first in range(0, query.shape[0], block_len):
            send_ref[target_ref[block]] = query[first : first + block_len]
            block += 1


def fetched_product(rows_ref, weights, stages, accs, sems):
    chunks = sems.shape[0]
    step = rows_ref.shape[1] // chunks

    def fetches(chunk):
        at = pl.ds(chunk * step, step)
        return [
            pltpu.make_async_copy(weight.at[at], stage.at[at], sems.at[chunk, k])
            for k, (weight, stage) in enumerate(zip(weights, stages))
        ]

    for chunk in range(chunks):
        for fetch in fetches(chunk):
            fetch.start()
    for chunk in range(chunks):
        for fetch in fetches(chunk):
            fetch.wait()
        at = slice(chunk * step, (chunk + 1) * step)
        for stage, acc in zip(stages, accs):
            product = jnp.dot(rows_ref[:, at], stage[at], preferred_element_type=jnp.float32)
            if chunk > 0:
                acc[...] += product
            else:
                acc[...] = product
    return [acc[...] for acc in accs]


def project_kernel(begin, carried, held, kind, fetch, after, *refs):
    refs = list(refs)
    target_ref = refs.pop(0) if kind == "routed" else None
    rows_ref = refs.pop(0)
    weights = [refs.pop(0), refs.pop(0)]
    given = [refs.pop(0), refs.pop(0)] if carried else None
    held_ref = refs.pop(0) if held else None
    refs = refs[after:]
    outs = [refs.pop(0), refs.pop(0)]
    if fetch:
        sums = fetched_product(rows_ref, weights, refs[:2], refs[2:4], refs[4])
    else:
        at = slice(begin, begin + rows_ref.shape[1])
        sums = [
            jnp.dot(rows_ref[...], weight[at], preferred_element_type=jnp.float32)
            for weight in weights
        ]
    if carried:
        sums = [ref[...] + product for ref, product in zip(given, sums)]
    if kind == "sums":
        for out, product in zip(outs, sums):
            out[...] = product
        return
    query, keyval = (product.astype(jnp.bfloat16) for product in sums)
    if kind == "routed":
        route(([held_ref[...]] if held else []) + [query], target_ref, outs[0])
    else:
        outs[0][...] = query
    outs[1][0] = keyval


def project(rows, weights, kind, begin=0, given=(), held=(), targets=(), slots=None, fetch=False, after=()):
    length, depth = rows.shape
    widths = [weight.shape[1] for weight in weights]
    columns = sum(widths)
    vmem = pl.BlockSpec(memory_space=pltpu.VMEM)
    if kind == "sums":
        shapes = [jax.ShapeDtypeStruct((length, width), jnp.float32) for width in widths]
    else:
        first = (*slots, widths[0]) if kind == "routed" else (length, widths[0])
        shapes = [
            jax.ShapeDtypeStruct(shape, jnp.bfloat16) for shape in (first, (1, length, widths[1]))
        ]
    scratch = []
    if fetch:
        scratch = [pltpu.VMEM((depth, width), jnp.bfloat16) for width in widths]
        scratch += [pltpu.VMEM((length, width), jnp.float32) for width in widths]
        scratch += [pltpu.SemaphoreType.DMA((math.gcd(depth // 256, 8), 2))]
    weight_spec = pl.BlockSpec(memory_space=pl.ANY) if fetch else vmem
    return pl.pallas_call(
        functools.partial(project_kernel, begin, bool(given), bool(held), kind, fetch, len(after)),
        out_shape=shapes,
        in_specs=[pl.BlockSpec(memory_space=pltpu.SMEM)] * len(targets)
        + [vmem, weight_spec, weight_spec]
        + [vmem] * (len(given) + len(held))
        + [pl.BlockSpec(memory_space=pl.ANY)] * len(after),
        out_specs=[vmem] * len(shapes),
        scratch_shapes=scratch,
        compiler_params=pltpu.CompilerParams(vmem_limit_bytes=(52 if fetch else 28) << 20),
        cost_estimate=pl.CostEstimate(
            flops=2 * length * depth * columns,
            bytes_accessed=2 * (length * depth + depth * columns + length * columns),
            transcendentals=0,
        ),
    )(*targets, rows, *weights, *given, *held, *after)


def touch_kernel(*refs):
    ref, out_ref = refs[0], refs[-1]
    out_ref[...] = ref[: out_ref.shape[0], : out_ref.shape[1]]


def touch(weights, *after):
    vmem = pl.BlockSpec(memory_space=pltpu.VMEM)
    hbm = pl.BlockSpec(memory_space=pl.ANY)
    return pl.pallas_call(
        touch_kernel,
        out_shape=jax.ShapeDtypeStruct((16, 128), weights[0].dtype),
        in_specs=[vmem] * len(weights) + [hbm] * len(after),
        out_specs=vmem,
        compiler_params=pltpu.CompilerParams(vmem_limit_bytes=20 << 20),
        name="touch",
    )(*weights, *after)


def gather_bits(count):
    bits = [1 << b for b in reversed(range(count.bit_length() - 1))]
    return bits[:1] + bits[2:3] + bits[1:2] + bits[3:]


def gather_all(part, count):
    pieces = [part]
    for bit in gather_bits(count):
        pairs = [(i, i ^ bit) for i in range(count)]
        held = pieces[0] if len(pieces) == 1 else jnp.concatenate(pieces, axis=0)
        pieces.append(lax.ppermute(held, "ctx", pairs))
    return pieces


def slots_of(refs):
    return [(ref, index) for ref in refs for index in range(ref.shape[0])]


def slot_source(slot, me, count):
    code = 0
    for place, bit in enumerate(gather_bits(count)):
        if slot >> place & 1:
            code |= bit
    return me ^ code


def attend_kernel(
    count,
    heads,
    segments,
    info_ref,
    source_ref,
    rank_ref,
    item_block_ref,
    item_tile_ref,
    start_ref,
    place_ref,
    arrived_refs,
    keyval_refs,
    out_ref,
    key_ref,
    value_ref,
    valt_ref,
    query_ref,
    max_ref,
    sum_ref,
    acc_ref,
):
    blocks, per_block = start_ref.shape
    block_len = arrived_refs[0].shape[1]
    dim = key_ref.shape[2]
    rows = key_ref.shape[1]
    me = info_ref[0]
    iterations = info_ref[1]
    own_place = info_ref[2]
    own_blocks = keyval_refs[0][0].shape[1] // block_len

    def place_rows(slots, piece_of, offset_at, first, length):
        row = pl.multiple_of(info_ref[offset_at] + first, 16)
        for slot in range(count):
            source = slot_source(slot, me, count)
            piece = piece_of(*slots[slot])
            key_ref[source, pl.ds(row, length), :] = piece[:, :dim]
            value_ref[source, pl.ds(row, length), :] = piece[:, dim:]

    for index, begin, offset_at, first, length in segments:
        place_rows(
            slots_of(keyval_refs[index]),
            lambda ref, slot: ref[slot, begin : begin + length, :],
            offset_at,
            first,
            length,
        )
    for tile in range(count):
        valt_ref[tile] = value_ref[tile].T

    for block in range(blocks):
        own = (block >= own_place) & (block < own_place + own_blocks)

        def take(ref, index):
            for head in range(heads):
                query_ref[block, head * block_len : (head + 1) * block_len, :] = ref[
                    index, :, head * dim : (head + 1) * dim
                ]

        @pl.when(own)
        def _():
            take(arrived_refs[0], source_ref[block])

        @pl.when(jnp.logical_not(own))
        def _():
            take(arrived_refs[1], source_ref[block])

    max_ref[...] = jnp.full_like(max_ref, NEG_FILL)
    sum_ref[...] = jnp.zeros_like(sum_ref)
    acc_ref[...] = jnp.zeros_like(acc_ref)
    key_index = lax.broadcasted_iota(jnp.int32, (rows, per_block), 0)
    scale = LOG2E / math.sqrt(dim)

    def step(iteration, carry):
        done = []
        for u in range(UNROLL):
            item = iteration * UNROLL + u
            block = item_block_ref[item]
            tile = item_tile_ref[item]
            safe = jnp.minimum(block, blocks - 1)
            scores = lax.dot_general(
                key_ref[tile],
                query_ref[safe],
                (((1,), (1,)), ((), ())),
                preferred_element_type=jnp.float32,
            )
            base = tile * rows
            start = start_ref[pl.ds(safe, 1), :] - base
            place = place_ref[pl.ds(safe, 1), :] - base
            allowed = (key_index >= start) & (key_index <= place)
            scores = jnp.where(allowed, scores * scale, NEG_FILL)
            highest = jnp.max(scores, axis=0, keepdims=True)
            weights = jnp.exp2(scores - highest)
            total = jnp.sum(weights, axis=0, keepdims=True)
            summed = lax.dot_general(
                valt_ref[tile],
                weights.astype(jnp.bfloat16),
                (((1,), (0,)), ((), ())),
                preferred_element_type=jnp.float32,
            )
            done.append((block, highest, total, summed))
        for block, highest, total, summed in done:
            old = max_ref[pl.ds(block, 1), :]
            new = jnp.maximum(old, highest)
            keep = jnp.exp2(old - new)
            add = jnp.exp2(highest - new)
            max_ref[pl.ds(block, 1), :] = new
            sum_ref[pl.ds(block, 1), :] = sum_ref[pl.ds(block, 1), :] * keep + total * add
            acc_ref[block] = acc_ref[block] * keep + summed * add
        return carry

    lax.fori_loop(0, iterations, step, 0)

    for block in range(blocks):
        result = (acc_ref[block] / sum_ref[block : block + 1, :]).T.astype(jnp.bfloat16)
        row = pl.multiple_of(rank_ref[block] * block_len, block_len)
        for head in range(heads):
            out_ref[pl.ds(row, block_len), head * dim : (head + 1) * dim] = result[
                head * block_len : (head + 1) * block_len, :
            ]


def step(tokens, query_weight, keyval_weight, doc_lengths, owners):
    count = lax.axis_size("ctx")
    me = lax.axis_index("ctx")
    groups = lax.axis_size("tp")
    member = lax.axis_index("tp")
    share, depth = tokens.shape
    rows = share * groups
    per = owners.shape[0] // count
    block_len = rows // per
    dim = keyval_weight.shape[1] // 2
    query_cols = query_weight.shape[1]
    heads = query_cols // dim
    share_blocks = share // block_len
    late = block_len * max(1, share_blocks // 2)
    rest = depth // 4

    pieces = [(shift, 0, share) for shift in range(1, groups - 1)]
    pieces += [(groups - 1, 0, share - late), (groups - 1, share - late, late)]
    head = min(16, pieces[0][2] // 2)

    def shifted(part, shift):
        return lax.ppermute(part, "tp", [(i, (i + shift) % groups) for i in range(groups)])

    grid = owners.reshape(count, per)
    place_of = jnp.arange(per, dtype=jnp.int32)
    sources = jnp.sum(
        jnp.where(grid == me, jnp.arange(count, dtype=jnp.int32)[:, None], 0), axis=0
    )
    mine = sources * per + place_of
    rank = jnp.sum((mine[None, :] < mine[:, None]).astype(jnp.int32), axis=1)
    length_count = doc_lengths.shape[0]
    order = jnp.arange(length_count)
    doc_ends = jnp.sum(
        jnp.where(order[None, :] <= order[:, None], doc_lengths[None, :], 0), axis=1
    )
    row_place = mine[:, None] * block_len + jnp.arange(block_len, dtype=jnp.int32)[None, :]
    row_start = jnp.max(
        jnp.where(doc_ends[None, None, :] <= row_place[:, :, None], doc_ends, 0), axis=2
    )
    first_tile = row_start[:, 0] // rows
    last_tile = row_place[:, -1] // rows
    tiles = last_tile - first_tile + 1
    before = jnp.sum(
        jnp.where(place_of[None, :] < place_of[:, None], tiles[None, :], 0), axis=1
    )
    item = jnp.arange(per * count + UNROLL, dtype=jnp.int32)
    within = (item[:, None] >= before[None, :]) & (item[:, None] < (before + tiles)[None, :])
    item_block = per - jnp.sum(jnp.where(within, per - place_of[None, :], 0), axis=1)
    item_tile = jnp.sum(
        jnp.where(within, first_tile[None, :] + item[:, None] - before[None, :], 0), axis=1
    )
    iterations = (jnp.sum(tiles) + UNROLL - 1) // UNROLL

    own_targets = lax.dynamic_index_in_dim(grid, me, 0, keepdims=False)

    def targets_of(shift, first, length):
        begin = ((member - shift) % groups) * share_blocks + first // block_len
        return lax.dynamic_slice_in_dim(own_targets, begin, length // block_len, 0)

    weights = (query_weight, keyval_weight)
    slots = (count, block_len)
    shift, first, length = pieces[0]
    early = [shifted(tokens[first : first + head], shift)]
    early.append(shifted(tokens[first + head : first + length], shift))
    for shift, first, length in pieces[1:-1]:
        early.append(shifted(tokens[first : first + length], shift))
    send_own, own_keyval = project(
        tokens, weights, "routed", targets=(targets_of(0, 0, share),), slots=slots, fetch=True
    )
    shift, first, length = pieces[-1]
    late_most = shifted(tokens[first : first + length, : depth - rest], shift)
    late_rest = shifted(tokens[first : first + length, depth - rest :], shift)
    gathered_own = gather_all(own_keyval, count)
    send_own, gathered_own[1] = lax.optimization_barrier((send_own, gathered_own[1]))
    arrived_own = lax.all_to_all(send_own, "ctx", 0, 0, tiled=True)
    early_rows = jnp.concatenate(early, axis=0)
    other_targets = jnp.concatenate([targets_of(*piece) for piece in pieces])
    touched = touch(weights, gathered_own[1], other_targets)
    early_query, early_keyval = project(early_rows, weights, "plain", after=(touched,))
    gathered_early = gather_all(early_keyval, count)
    sums = project(late_most, weights, "sums")
    send_other, late_keyval = project(
        late_rest,
        weights,
        "routed",
        begin=depth - rest,
        given=sums,
        held=(early_query,),
        targets=(other_targets,),
        slots=slots,
    )
    gathered_late = gather_all(late_keyval, count)
    arrived_other = lax.all_to_all(send_other, "ctx", 0, 0, tiled=True)

    segments = [(0, 0, 3, 0, share)]
    begin = 0
    for shift, first, length in pieces[:-1]:
        segments.append((1, begin, 3 + shift, first, length))
        begin += length
    segments.append((2, 0, 3 + pieces[-1][0], pieces[-1][1], late))
    offsets = [((member - shift) % groups) * share for shift in range(groups)]

    info = jnp.stack([me, iterations, member * share_blocks, *offsets]).astype(jnp.int32)
    per_block = heads * block_len
    smem = pl.BlockSpec(memory_space=pltpu.SMEM)
    vmem = pl.BlockSpec(memory_space=pltpu.VMEM)
    return pl.pallas_call(
        functools.partial(attend_kernel, count, heads, tuple(segments)),
        out_shape=jax.ShapeDtypeStruct((rows, query_cols), jnp.bfloat16),
        in_specs=[smem] * 5 + [vmem] * 2 + [[vmem] * 2, [[vmem] * len(gathered_late)] * 3],
        out_specs=vmem,
        scratch_shapes=[
            pltpu.VMEM((count, rows, dim), jnp.bfloat16),
            pltpu.VMEM((count, rows, dim), jnp.bfloat16),
            pltpu.VMEM((count, dim, rows), jnp.bfloat16),
            pltpu.VMEM((per, per_block, dim), jnp.bfloat16),
            pltpu.VMEM((per + 1, per_block), jnp.float32),
            pltpu.VMEM((per + 1, per_block), jnp.float32),
            pltpu.VMEM((per + 1, dim, per_block), jnp.float32),
        ],
        compiler_params=pltpu.CompilerParams(vmem_limit_bytes=16 << 20),
        name="attend",
    )(
        info,
        sources,
        rank,
        item_block,
        item_tile,
        jnp.tile(row_start, (1, heads)),
        jnp.tile(row_place, (1, heads)),
        [arrived_own, arrived_other],
        [gathered_own, gathered_early, gathered_late],
    )


def solution(mesh):
    return jax.shard_map(
        step,
        mesh=mesh,
        in_specs=(P(("ctx", "tp"), None), P(None, "tp"), P(None, "tp"), P(), P()),
        out_specs=P("ctx", "tp"),
        check_vma=False,
    )
```

profile of v0, /device:TPU:0, one launch (start us, length us, event | category | flops | bytes accessed | tf_op | source)
XLA Modules:
  0.0 100.9 jit_solution(11978564921275241652)
XLA Ops:
  0.8 7.5 %shard_map.55 = (bf16[16,32,512]{2,1,0:T(8,128)(2,1)}, bf16[1,128,256]{2,1,0:T(8,128)(2,1)S(1)}) custom-call(s32[4]{0:T(128)S(1)} %dynamic-slice_bitcast_fusion.2.refs_0_, bf16[128,8192]{1,0:T(8,128)(2,1)} %refs_1_.4, bf16[8192,512]{1,0:T(8,128)(2,1)} %refs_2_.7, bf16[8192,256]{1,0:T(8,128)(2,1)} %refs_3_.3), custom_call_target="tpu_custom_call" | custom-call | flops 1610612736 | bytes 14876672 | tf_op jit(solution)/shard_map/pallas_call | solution.py:102
  8.4 4.1 %collective-permute-start = (bf16[1,128,256]{2,1,0:T(8,128)(2,1)S(1)}, bf16[1,128,256]{2,1,0:T(8,128)(2,1)S(1)}, u32[]{:S(2)}, u32[]{:S(2)}) collective-permute-start(bf16[1,128,256]{2,1,0:T(8,128)(2,1)S(1)} %get-tuple-element.16.keyval_refs_0__0_), channel_id=1, source_target_pairs={{0,16},{2,18},{4,20},{6,22},{8,24},{10,26},{12,28},{14,30},{16,0},... | collective-permute-start | bytes 196616 | tf_op jit(solution)/shard_map/ppermute | solution.py:148
  12.5 1.6 %collective-permute-start.1 = (bf16[64,2048]{1,0:T(8,128)(2,1)S(1)}, bf16[64,2048]{1,0:T(8,128)(2,1)S(1)}, u32[]{:S(2)}, u32[]{:S(2)}) collective-permute-start(bf16[64,2048]{1,0:T(8,128)(2,1)S(1)} %slice.20), channel_id=1, source_target_pairs={{0,1},{1,0},{2,3},{3,2},{4,5},{5,4},{6,7},{7,6},{8,9},{9,8},{10,11... | collective-permute-start | bytes 786440 | tf_op jit(solution)/shard_map/ppermute | solution.py:307
  15.7 1.5 %collective-permute-start.4 = (bf16[48,8192]{1,0:T(8,128)(2,1)}, bf16[48,8192]{1,0:T(8,128)(2,1)}, u32[]{:S(2)}, u32[]{:S(2)}) collective-permute-start(bf16[48,8192]{1,0:T(8,128)(2,1)} %slice.23), channel_id=1, source_target_pairs={{0,1},{1,0},{2,3},{3,2},{4,5},{5,4},{6,7},{7,6},{8,9},{9,8},{10,11... | collective-permute-start | bytes 2359304 | tf_op jit(solution)/shard_map/ppermute | solution.py:307
  20.1 1.6 %collective-permute-start.5 = (bf16[2,128,256]{2,1,0:T(8,128)(2,1)S(1)}, bf16[2,128,256]{2,1,0:T(8,128)(2,1)S(1)}, u32[]{:S(2)}, u32[]{:S(2)}) collective-permute-start(bf16[2,128,256]{2,1,0:T(8,128)(2,1)S(1)} %pad_maximum_fusion.5), channel_id=1, source_target_pairs={{0,4},{2,6},{4,0},{6,2},{8,12},{10,14},{12,8},{14,10},{16,20},{18,... | collective-permute-start | bytes 393224 | tf_op jit(solution)/shard_map/ppermute | solution.py:148
  21.9 3.6 %all-to-all-start = ((bf16[16,32,512]{2,1,0:T(8,128)(2,1)}), bf16[16,32,512]{2,1,0:T(8,128)(2,1)S(1)}, u32[]{:S(2)}, u32[]{:S(2)}) async-start(bf16[16,32,512]{2,1,0:T(8,128)(2,1)} %get-tuple-element.17), calls=%async_computation | async-start | bytes 1048576 | tf_op jit(solution)/shard_map/all_to_all | solution.py:360
  25.5 3.4 %copy-done = bf16[8192,512]{1,0:T(8,128)(2,1)S(1)} copy-done((bf16[8192,512]{1,0:T(8,128)(2,1)S(1)}, bf16[8192,512]{1,0:T(8,128)(2,1)}, u32[]{:S(2)}) %copy-start) | copy-done | bytes 8388632
  28.8 2.2 %copy-done.2 = bf16[8192,256]{1,0:T(8,128)(2,1)S(1)} copy-done((bf16[8192,256]{1,0:T(8,128)(2,1)S(1)}, bf16[8192,256]{1,0:T(8,128)(2,1)}, u32[]{:S(2)}) %copy-start.2) | copy-done | bytes 4194328
  31.8 1.8 %collective-permute-start.6 = (bf16[4,128,256]{2,1,0:T(8,128)(2,1)}, bf16[4,128,256]{2,1,0:T(8,128)(2,1)S(1)}, u32[]{:S(2)}, u32[]{:S(2)}) collective-permute-start(bf16[4,128,256]{2,1,0:T(8,128)(2,1)} %pad_maximum_fusion.2), channel_id=1, source_target_pairs={{0,8},{2,10},{4,12},{6,14},{8,0},{10,2},{12,4},{14,6},{16,24},{18,... | collective-permute-start | bytes 786440 | tf_op jit(solution)/shard_map/ppermute | solution.py:148
  33.6 26.2 %collective-permute-done.3 = bf16[16,8192]{1,0:T(8,128)(2,1)} collective-permute-done((bf16[16,8192]{1,0:T(8,128)(2,1)}, bf16[16,8192]{1,0:T(8,128)(2,1)}, u32[]{:S(2)}, u32[]{:S(2)}) %collective-permute-start.3) | collective-permute-done | bytes 262176 | tf_op jit(solution)/shard_map/ppermute | solution.py:307
  59.8 1.3 %pad_maximum_fusion.refs_0_ = bf16[64,8192]{1,0:T(8,128)(2,1)S(1)} fusion(bf16[48,8192]{1,0:T(8,128)(2,1)} %collective-permute-done.4, bf16[16,8192]{1,0:T(8,128)(2,1)} %collective-permute-done.3), kind=kLoop, calls=%fused_computation | loop fusion | flops 2097152 | bytes 2097152 | tf_op jit(solution)/shard_map/concatenate | solution.py:361
  61.1 2.3 %shard_map.57 = (bf16[64,512]{1,0:T(8,128)(2,1)S(1)}, bf16[1,64,256]{2,1,0:T(8,128)(2,1)S(1)}) custom-call(bf16[64,8192]{1,0:T(8,128)(2,1)S(1)} %pad_maximum_fusion.refs_0_, bf16[8192,512]{1,0:T(8,128)(2,1)S(1)} %copy-done.1, bf16[8192,256]{1,0:T(8,128)(2,1)S(1)} %copy-done.2, bf16[16,128]{1,0:T(8,128)(2,1)S(1)} %touch.1.refs_3_), custom_call_target="tpu_custom_call" | custom-call | flops 805306368 | bytes 13729792 | tf_op jit(solution)/shard_map/pallas_call | solution.py:102
  63.8 1.8 %shard_map.56 = (f32[64,512]{1,0:T(8,128)S(1)}, f32[64,256]{1,0:T(8,128)S(1)}) custom-call(bf16[64,6144]{1,0:T(8,128)(2,1)S(1)} %collective-permute-done.2.refs_0_, bf16[8192,512]{1,0:T(8,128)(2,1)S(1)} %copy-done.1, bf16[8192,256]{1,0:T(8,128)(2,1)S(1)} %copy-done.2), custom_call_target="tpu_custom_call" | custom-call | flops 603979776 | bytes 10321920 | tf_op jit(solution)/shard_map/pallas_call | solution.py:102
  65.5 2.0 %shard_map.58 = (bf16[16,32,512]{2,1,0:T(8,128)(2,1)}, bf16[1,64,256]{2,1,0:T(8,128)(2,1)S(1)}) custom-call(s32[4]{0:T(128)S(1)} %pad_add_fusion.refs_3_.refs_0_, bf16[64,2048]{1,0:T(8,128)(2,1)S(1)} %collective-permute-done.1.refs_1_, bf16[8192,512]{1,0:T(8,128)(2,1)S(1)} %copy-done.1, bf16[8192,256]{1,0:T(8,128)(2,1)S(1)} %copy-done.2, ...), custom_call_target="tpu_custom_call" | custom-call | flops 201326592 | bytes 3506176 | tf_op jit(solution)/shard_map/pallas_call | solution.py:102
  67.5 2.6 %collective-permute-start.12 = (bf16[1,64,256]{2,1,0:T(8,128)(2,1)S(1)}, bf16[1,64,256]{2,1,0:T(8,128)(2,1)S(1)}, u32[]{:S(2)}, u32[]{:S(2)}) collective-permute-start(bf16[1,64,256]{2,1,0:T(8,128)(2,1)S(1)} %get-tuple-element.24.keyval_refs_2__0_), channel_id=1, source_target_pairs={{0,16},{2,18},{4,20},{6,22},{8,24},{10,26},{12,28},{14,30},{16,0},... | collective-permute-start | bytes 98312 | tf_op jit(solution)/shard_map/ppermute | solution.py:148
  70.2 1.6 %collective-permute-start.9 = (bf16[2,64,256]{2,1,0:T(8,128)(2,1)S(1)}, bf16[2,64,256]{2,1,0:T(8,128)(2,1)S(1)}, u32[]{:S(2)}, u32[]{:S(2)}) collective-permute-start(bf16[2,64,256]{2,1,0:T(8,128)(2,1)S(1)} %pad_maximum_fusion.8), channel_id=1, source_target_pairs={{0,4},{2,6},{4,0},{6,2},{8,12},{10,14},{12,8},{14,10},{16,20},{18,... | collective-permute-start | bytes 196616 | tf_op jit(solution)/shard_map/ppermute | solution.py:148
  71.8 3.6 %all-to-all-start.1 = ((bf16[16,32,512]{2,1,0:T(8,128)(2,1)}), bf16[16,32,512]{2,1,0:T(8,128)(2,1)S(1)}, u32[]{:S(2)}, u32[]{:S(2)}) async-start(bf16[16,32,512]{2,1,0:T(8,128)(2,1)} %get-tuple-element.22), calls=%async_computation.1 | async-start | bytes 1048576 | tf_op jit(solution)/shard_map/all_to_all | solution.py:378
  75.4 1.9 %collective-permute-start.13 = (bf16[2,64,256]{2,1,0:T(8,128)(2,1)S(1)}, bf16[2,64,256]{2,1,0:T(8,128)(2,1)S(1)}, u32[]{:S(2)}, u32[]{:S(2)}) collective-permute-start(bf16[2,64,256]{2,1,0:T(8,128)(2,1)S(1)} %pad_maximum_fusion.9), channel_id=1, source_target_pairs={{0,4},{2,6},{4,0},{6,2},{8,12},{10,14},{12,8},{14,10},{16,20},{18,... | collective-permute-start | bytes 196616 | tf_op jit(solution)/shard_map/ppermute | solution.py:148
  77.3 1.6 %collective-permute-start.10 = (bf16[4,64,256]{2,1,0:T(8,128)(2,1)S(1)}, bf16[4,64,256]{2,1,0:T(8,128)(2,1)S(1)}, u32[]{:S(2)}, u32[]{:S(2)}) collective-permute-start(bf16[4,64,256]{2,1,0:T(8,128)(2,1)S(1)} %pad_maximum_fusion.6), channel_id=1, source_target_pairs={{0,8},{2,10},{4,12},{6,14},{8,0},{10,2},{12,4},{14,6},{16,24},{18,... | collective-permute-start | bytes 393224 | tf_op jit(solution)/shard_map/ppermute | solution.py:148
  78.8 4.0 %collective-permute-done.13.keyval_refs_2__2_ = bf16[2,64,256]{2,1,0:T(8,128)(2,1)S(1)} collective-permute-done((bf16[2,64,256]{2,1,0:T(8,128)(2,1)S(1)}, bf16[2,64,256]{2,1,0:T(8,128)(2,1)S(1)}, u32[]{:S(2)}, u32[]{:S(2)}) %collective-permute-start.13) | collective-permute-done | bytes 65568 | tf_op jit(solution)/shard_map/ppermute | solution.py:148
  82.8 1.3 %collective-permute-start.14 = (bf16[4,64,256]{2,1,0:T(8,128)(2,1)S(1)}, bf16[4,64,256]{2,1,0:T(8,128)(2,1)S(1)}, u32[]{:S(2)}, u32[]{:S(2)}) collective-permute-start(bf16[4,64,256]{2,1,0:T(8,128)(2,1)S(1)} %pad_maximum_fusion.7), channel_id=1, source_target_pairs={{0,8},{2,10},{4,12},{6,14},{8,0},{10,2},{12,4},{14,6},{16,24},{18,... | collective-permute-start | bytes 393224 | tf_op jit(solution)/shard_map/ppermute | solution.py:148
  84.9 5.2 %collective-permute-done.10.keyval_refs_1__3_ = bf16[4,64,256]{2,1,0:T(8,128)(2,1)S(1)} collective-permute-done((bf16[4,64,256]{2,1,0:T(8,128)(2,1)S(1)}, bf16[4,64,256]{2,1,0:T(8,128)(2,1)S(1)}, u32[]{:S(2)}, u32[]{:S(2)}) %collective-permute-start.10) | collective-permute-done | bytes 131104 | tf_op jit(solution)/shard_map/ppermute | solution.py:148
  90.3 2.1 %collective-permute-done.14.keyval_refs_2__3_ = bf16[4,64,256]{2,1,0:T(8,128)(2,1)S(1)} collective-permute-done((bf16[4,64,256]{2,1,0:T(8,128)(2,1)S(1)}, bf16[4,64,256]{2,1,0:T(8,128)(2,1)S(1)}, u32[]{:S(2)}, u32[]{:S(2)}) %collective-permute-start.14) | collective-permute-done | bytes 131104 | tf_op jit(solution)/shard_map/ppermute | solution.py:148
  94.9 6.1 %attend.1 = bf16[256,512]{1,0:T(8,128)(2,1)} custom-call(s32[5]{0:T(128)S(1)} %stack.23.info_ref, s32[8]{0:T(128)S(1)} %select_reduce_fusion.4.source_ref, s32[8]{0:T(128)S(1)} %convert_reduce_fusion.rank_ref, s32[136]{0:T(256)S(1)} %broadcast_subtract_fusion.item_block_ref, s32[136]{0:T(256)S(1)} %get-tuple-element.25.item_tile_ref, ...), custom_call_target="tpu_custom_call" | custom-call | tf_op jit(solution)/shard_map/attend/pallas_call | solution.py:392
  (64 shorter events, 9.4 us)
Async XLA Ops:
  0.8 11.7 %copy-start.3 = (bf16[128,8192]{1,0:T(8,128)(2,1)S(1)}, bf16[128,8192]{1,0:T(8,128)(2,1)}, u32[]{:S(2)}) copy-start(bf16[128,8192]{1,0:T(8,128)(2,1)} %refs_1_.4) | copy-start | bytes 6291460
  8.4 10.2 %copy-start.4 = (s32[32]{0:T(128)S(1)}, s32[32]{0:T(128)}, u32[]{:S(2)}) copy-start(s32[32]{0:T(128)} %param.8) | copy-start | bytes 388
  8.4 11.7 %collective-permute-start = (bf16[1,128,256]{2,1,0:T(8,128)(2,1)S(1)}, bf16[1,128,256]{2,1,0:T(8,128)(2,1)S(1)}, u32[]{:S(2)}, u32[]{:S(2)}) collective-permute-start(bf16[1,128,256]{2,1,0:T(8,128)(2,1)S(1)} %get-tuple-element.16.keyval_refs_0__0_), channel_id=1, source_target_pairs={{0,16},{2,18},{4,20},{6,22},{8,24},{10,26},{12,28},{14,30},{16,0},... | collective-permute-start | bytes 196616 | tf_op jit(solution)/shard_map/ppermute | solution.py:148
  12.5 53.0 %collective-permute-start.1 = (bf16[64,2048]{1,0:T(8,128)(2,1)S(1)}, bf16[64,2048]{1,0:T(8,128)(2,1)S(1)}, u32[]{:S(2)}, u32[]{:S(2)}) collective-permute-start(bf16[64,2048]{1,0:T(8,128)(2,1)S(1)} %slice.20), channel_id=1, source_target_pairs={{0,1},{1,0},{2,3},{3,2},{4,5},{5,4},{6,7},{7,6},{8,9},{9,8},{10,11... | collective-permute-start | bytes 786440 | tf_op jit(solution)/shard_map/ppermute | solution.py:307
  14.1 49.6 %collective-permute-start.2 = (bf16[64,6144]{1,0:T(8,128)(2,1)S(1)}, bf16[64,6144]{1,0:T(8,128)(2,1)S(1)}, u32[]{:S(2)}, u32[]{:S(2)}) collective-permute-start(bf16[64,6144]{1,0:T(8,128)(2,1)S(1)} %slice.21), channel_id=1, source_target_pairs={{0,1},{1,0},{2,3},{3,2},{4,5},{5,4},{6,7},{7,6},{8,9},{9,8},{10,11... | collective-permute-start | bytes 2359304 | tf_op jit(solution)/shard_map/ppermute | solution.py:307
  15.7 44.1 %collective-permute-start.4 = (bf16[48,8192]{1,0:T(8,128)(2,1)}, bf16[48,8192]{1,0:T(8,128)(2,1)}, u32[]{:S(2)}, u32[]{:S(2)}) collective-permute-start(bf16[48,8192]{1,0:T(8,128)(2,1)} %slice.23), channel_id=1, source_target_pairs={{0,1},{1,0},{2,3},{3,2},{4,5},{5,4},{6,7},{7,6},{8,9},{9,8},{10,11... | collective-permute-start | bytes 2359304 | tf_op jit(solution)/shard_map/ppermute | solution.py:307
  17.9 41.9 %collective-permute-start.3 = (bf16[16,8192]{1,0:T(8,128)(2,1)}, bf16[16,8192]{1,0:T(8,128)(2,1)}, u32[]{:S(2)}, u32[]{:S(2)}) collective-permute-start(bf16[16,8192]{1,0:T(8,128)(2,1)} %slice.22), channel_id=1, source_target_pairs={{0,1},{1,0},{2,3},{3,2},{4,5},{5,4},{6,7},{7,6},{8,9},{9,8},{10,11... | collective-permute-start | bytes 786440 | tf_op jit(solution)/shard_map/ppermute | solution.py:307
  20.1 10.9 %collective-permute-start.5 = (bf16[2,128,256]{2,1,0:T(8,128)(2,1)S(1)}, bf16[2,128,256]{2,1,0:T(8,128)(2,1)S(1)}, u32[]{:S(2)}, u32[]{:S(2)}) collective-permute-start(bf16[2,128,256]{2,1,0:T(8,128)(2,1)S(1)} %pad_maximum_fusion.5), channel_id=1, source_target_pairs={{0,4},{2,6},{4,0},{6,2},{8,12},{10,14},{12,8},{14,10},{16,20},{18,... | collective-permute-start | bytes 393224 | tf_op jit(solution)/shard_map/ppermute | solution.py:148
  21.9 49.9 %all-to-all-start = ((bf16[16,32,512]{2,1,0:T(8,128)(2,1)}), bf16[16,32,512]{2,1,0:T(8,128)(2,1)S(1)}, u32[]{:S(2)}, u32[]{:S(2)}) async-start(bf16[16,32,512]{2,1,0:T(8,128)(2,1)} %get-tuple-element.17), calls=%async_computation | async-start | bytes 1048576 | tf_op jit(solution)/shard_map/all_to_all | solution.py:360
  25.4 3.4 %copy-start = (bf16[8192,512]{1,0:T(8,128)(2,1)S(1)}, bf16[8192,512]{1,0:T(8,128)(2,1)}, u32[]{:S(2)}) copy-start(bf16[8192,512]{1,0:T(8,128)(2,1)} %refs_2_.7) | copy-start | bytes 25165828
  28.8 2.2 %copy-start.2 = (bf16[8192,256]{1,0:T(8,128)(2,1)S(1)}, bf16[8192,256]{1,0:T(8,128)(2,1)}, u32[]{:S(2)}) copy-start(bf16[8192,256]{1,0:T(8,128)(2,1)} %refs_3_.3) | copy-start | bytes 12582916
  31.0 30.0 %copy-start.1 = (bf16[8192,512]{1,0:T(8,128)(2,1)S(1)}, bf16[8192,512]{1,0:T(8,128)(2,1)}, u32[]{:S(2)}) copy-start(bf16[8192,512]{1,0:T(8,128)(2,1)} %refs_2_.7) | copy-start | bytes 25165828
  31.8 52.3 %collective-permute-start.6 = (bf16[4,128,256]{2,1,0:T(8,128)(2,1)}, bf16[4,128,256]{2,1,0:T(8,128)(2,1)S(1)}, u32[]{:S(2)}, u32[]{:S(2)}) collective-permute-start(bf16[4,128,256]{2,1,0:T(8,128)(2,1)} %pad_maximum_fusion.2), channel_id=1, source_target_pairs={{0,8},{2,10},{4,12},{6,14},{8,0},{10,2},{12,4},{14,6},{16,24},{18,... | collective-permute-start | bytes 786440 | tf_op jit(solution)/shard_map/ppermute | solution.py:148
  63.4 6.8 %collective-permute-start.8 = (bf16[1,64,256]{2,1,0:T(8,128)(2,1)S(1)}, bf16[1,64,256]{2,1,0:T(8,128)(2,1)S(1)}, u32[]{:S(2)}, u32[]{:S(2)}) collective-permute-start(bf16[1,64,256]{2,1,0:T(8,128)(2,1)S(1)} %get-tuple-element.23.keyval_refs_1__0_), channel_id=1, source_target_pairs={{0,16},{2,18},{4,20},{6,22},{8,24},{10,26},{12,28},{14,30},{16,0},... | collective-permute-start | bytes 98312 | tf_op jit(solution)/shard_map/ppermute | solution.py:148
  67.5 7.8 %collective-permute-start.12 = (bf16[1,64,256]{2,1,0:T(8,128)(2,1)S(1)}, bf16[1,64,256]{2,1,0:T(8,128)(2,1)S(1)}, u32[]{:S(2)}, u32[]{:S(2)}) collective-permute-start(bf16[1,64,256]{2,1,0:T(8,128)(2,1)S(1)} %get-tuple-element.24.keyval_refs_2__0_), channel_id=1, source_target_pairs={{0,16},{2,18},{4,20},{6,22},{8,24},{10,26},{12,28},{14,30},{16,0},... | collective-permute-start | bytes 98312 | tf_op jit(solution)/shard_map/ppermute | solution.py:148
  70.2 7.1 %collective-permute-start.9 = (bf16[2,64,256]{2,1,0:T(8,128)(2,1)S(1)}, bf16[2,64,256]{2,1,0:T(8,128)(2,1)S(1)}, u32[]{:S(2)}, u32[]{:S(2)}) collective-permute-start(bf16[2,64,256]{2,1,0:T(8,128)(2,1)S(1)} %pad_maximum_fusion.8), channel_id=1, source_target_pairs={{0,4},{2,6},{4,0},{6,2},{8,12},{10,14},{12,8},{14,10},{16,20},{18,... | collective-permute-start | bytes 196616 | tf_op jit(solution)/shard_map/ppermute | solution.py:148
  71.8 23.1 %all-to-all-start.1 = ((bf16[16,32,512]{2,1,0:T(8,128)(2,1)}), bf16[16,32,512]{2,1,0:T(8,128)(2,1)S(1)}, u32[]{:S(2)}, u32[]{:S(2)}) async-start(bf16[16,32,512]{2,1,0:T(8,128)(2,1)} %get-tuple-element.22), calls=%async_computation.1 | async-start | bytes 1048576 | tf_op jit(solution)/shard_map/all_to_all | solution.py:378
  75.4 7.4 %collective-permute-start.13 = (bf16[2,64,256]{2,1,0:T(8,128)(2,1)S(1)}, bf16[2,64,256]{2,1,0:T(8,128)(2,1)S(1)}, u32[]{:S(2)}, u32[]{:S(2)}) collective-permute-start(bf16[2,64,256]{2,1,0:T(8,128)(2,1)S(1)} %pad_maximum_fusion.9), channel_id=1, source_target_pairs={{0,4},{2,6},{4,0},{6,2},{8,12},{10,14},{12,8},{14,10},{16,20},{18,... | collective-permute-start | bytes 196616 | tf_op jit(solution)/shard_map/ppermute | solution.py:148
  77.3 12.9 %collective-permute-start.10 = (bf16[4,64,256]{2,1,0:T(8,128)(2,1)S(1)}, bf16[4,64,256]{2,1,0:T(8,128)(2,1)S(1)}, u32[]{:S(2)}, u32[]{:S(2)}) collective-permute-start(bf16[4,64,256]{2,1,0:T(8,128)(2,1)S(1)} %pad_maximum_fusion.6), channel_id=1, source_target_pairs={{0,8},{2,10},{4,12},{6,14},{8,0},{10,2},{12,4},{14,6},{16,24},{18,... | collective-permute-start | bytes 393224 | tf_op jit(solution)/shard_map/ppermute | solution.py:148
  82.8 9.6 %collective-permute-start.14 = (bf16[4,64,256]{2,1,0:T(8,128)(2,1)S(1)}, bf16[4,64,256]{2,1,0:T(8,128)(2,1)S(1)}, u32[]{:S(2)}, u32[]{:S(2)}) collective-permute-start(bf16[4,64,256]{2,1,0:T(8,128)(2,1)S(1)} %pad_maximum_fusion.7), channel_id=1, source_target_pairs={{0,8},{2,10},{4,12},{6,14},{8,0},{10,2},{12,4},{14,6},{16,24},{18,... | collective-permute-start | bytes 393224 | tf_op jit(solution)/shard_map/ppermute | solution.py:148
  84.9 9.3 %collective-permute-start.7 = (bf16[8,128,256]{2,1,0:T(8,128)(2,1)}, bf16[8,128,256]{2,1,0:T(8,128)(2,1)S(1)}, u32[]{:S(2)}, u32[]{:S(2)}) collective-permute-start(bf16[8,128,256]{2,1,0:T(8,128)(2,1)} %pad_maximum_fusion.1), channel_id=1, source_target_pairs={{0,2},{2,0},{4,6},{6,4},{8,10},{10,8},{12,14},{14,12},{16,18},{18,... | collective-permute-start | bytes 1572872 | tf_op jit(solution)/shard_map/ppermute | solution.py:148
  90.2 4.1 %collective-permute-start.11 = (bf16[8,64,256]{2,1,0:T(8,128)(2,1)S(1)}, bf16[8,64,256]{2,1,0:T(8,128)(2,1)S(1)}, u32[]{:S(2)}, u32[]{:S(2)}) collective-permute-start(bf16[8,64,256]{2,1,0:T(8,128)(2,1)S(1)} %pad_maximum_fusion.3), channel_id=1, source_target_pairs={{0,2},{2,0},{4,6},{6,4},{8,10},{10,8},{12,14},{14,12},{16,18},{18,... | collective-permute-start | bytes 786440 | tf_op jit(solution)/shard_map/ppermute | solution.py:148
  93.1 1.7 %collective-permute-start.15 = (bf16[8,64,256]{2,1,0:T(8,128)(2,1)}, bf16[8,64,256]{2,1,0:T(8,128)(2,1)S(1)}, u32[]{:S(2)}, u32[]{:S(2)}) collective-permute-start(bf16[8,64,256]{2,1,0:T(8,128)(2,1)} %pad_maximum_fusion.4), channel_id=1, source_target_pairs={{0,2},{2,0},{4,6},{6,4},{8,10},{10,8},{12,14},{14,12},{16,18},{18,... | collective-permute-start | bytes 786440 | tf_op jit(solution)/shard_map/ppermute | solution.py:148
where the time goes:
time: 101 us
  waiting for transfers between devices  38.2 us (38%)
  starting transfers between devices  28.2 us (28%)
  Pallas kernels  19.7 us (20%)
  local copies, waits for them, and re-layouts  8.62 us (9%)
  other arithmetic  5.35 us (5%)
    ppermute x4, waiting for transfers between devices, shifted(): lax.ppermute(part, 'tp', [(i, (i + shift) % groups) for i in range(groups)])  26.2 us
    ppermute x12, starting transfers between devices, gather_all(): pieces.append(lax.ppermute(held, 'ctx', pairs))  16.9 us
    pallas_call x4, Pallas kernels, project(): pl.pallas_call(functools.partial(project_kernel, begin, bool(given), bool...  13.6 us
    ppermute x12, waiting for transfers between devices, gather_all(): pieces.append(lax.ppermute(held, 'ctx', pairs))  11.9 us
    pallas_call x1, Pallas kernels, step(): pl.pallas_call(functools.partial(attend_kernel, count, heads, tuple(segme...  6.06 us
    unnamed x10, local copies, waits for them, and re-layouts  5.58 us
    ppermute x4, starting transfers between devices, shifted(): lax.ppermute(part, 'tp', [(i, (i + shift) % groups) for i in range(groups)])  4.18 us
    all_to_all x1, starting transfers between devices, step(): arrived_own = lax.all_to_all(send_own, 'ctx', 0, 0, tiled=True)  3.58 us
  transfers between devices with their start and end apart: 18, of which 5 were waited for; matrix products, arithmetic and copies ran while one was open for 8% of the time, Pallas kernels for 6%

commit v1 on v0

--- a/solution.py
+++ b/solution.py
@@ -16,11 +16,14 @@
 
 def route(queries, target_ref, send_ref):
     block_len = send_ref.shape[1]
-    block = 0
+    row = 0
     for query in queries:
-        for first in range(0, query.shape[0], block_len):
-            send_ref[target_ref[block]] = query[first : first + block_len]
-            block += 1
+        first = 0
+        while first < query.shape[0]:
+            block, at = divmod(row, block_len)
+            length = min(block_len - at, query.shape[0] - first)
+            send_ref[target_ref[block], at : at + length] = query[first : first + length]
+            first, row = first + length, row + length
 
 
 def fetched_product(rows_ref, weights, stages, accs, sems):
@@ -50,21 +53,22 @@
     return [acc[...] for acc in accs]
 
 
-def project_kernel(begin, carried, held, kind, fetch, after, *refs):
+def project_kernel(parts, begin, carried, held, kind, fetch, after, *refs):
     refs = list(refs)
     target_ref = refs.pop(0) if kind == "routed" else None
-    rows_ref = refs.pop(0)
+    row_refs = [refs.pop(0) for _ in range(parts)]
     weights = [refs.pop(0), refs.pop(0)]
     given = [refs.pop(0), refs.pop(0)] if carried else None
     held_ref = refs.pop(0) if held else None
     refs = refs[after:]
     outs = [refs.pop(0), refs.pop(0)]
     if fetch:
-        sums = fetched_product(rows_ref, weights, refs[:2], refs[2:4], refs[4])
+        sums = fetched_product(row_refs[0], weights, refs[:2], refs[2:4], refs[4])
     else:
-        at = slice(begin, begin + rows_ref.shape[1])
+        rows = jnp.concatenate([ref[...] for ref in row_refs], axis=0)
+        at = slice(begin, begin + rows.shape[1])
         sums = [
-            jnp.dot(rows_ref[...], weight[at], preferred_element_type=jnp.float32)
+            jnp.dot(rows, weight[at], preferred_element_type=jnp.float32)
             for weight in weights
         ]
     if carried:
@@ -81,8 +85,8 @@
     outs[1][0] = keyval
 
 
-def project(rows, weights, kind, begin=0, given=(), held=(), targets=(), slots=None, fetch=False, after=()):
-    length, depth = rows.shape
+def project(row_parts, weights, kind, begin=0, given=(), held=(), targets=(), slots=None, fetch=False, after=()):
+    length, depth = sum(rows.shape[0] for rows in row_parts), row_parts[0].shape[1]
     widths = [weight.shape[1] for weight in weights]
     columns = sum(widths)
     vmem = pl.BlockSpec(memory_space=pltpu.VMEM)
@@ -100,10 +104,13 @@
         scratch += [pltpu.SemaphoreType.DMA((math.gcd(depth // 256, 8), 2))]
     weight_spec = pl.BlockSpec(memory_space=pl.ANY) if fetch else vmem
     return pl.pallas_call(
-        functools.partial(project_kernel, begin, bool(given), bool(held), kind, fetch, len(after)),
+        functools.partial(
+            project_kernel, len(row_parts), begin, bool(given), bool(held), kind, fetch, len(after)
+        ),
         out_shape=shapes,
         in_specs=[pl.BlockSpec(memory_space=pltpu.SMEM)] * len(targets)
-        + [vmem, weight_spec, weight_spec]
+        + [vmem] * len(row_parts)
+        + [weight_spec] * 2
         + [vmem] * (len(given) + len(held))
         + [pl.BlockSpec(memory_space=pl.ANY)] * len(after),
         out_specs=[vmem] * len(shapes),
@@ -114,7 +121,7 @@
             bytes_accessed=2 * (length * depth + depth * columns + length * columns),
             transcendentals=0,
         ),
-    )(*targets, rows, *weights, *given, *held, *after)
+    )(*targets, *row_parts, *weights, *given, *held, *after)
 
 
 def touch_kernel(*refs):
@@ -130,7 +137,10 @@
         out_shape=jax.ShapeDtypeStruct((16, 128), weights[0].dtype),
         in_specs=[vmem] * len(weights) + [hbm] * len(after),
         out_specs=vmem,
-        compiler_params=pltpu.CompilerParams(vmem_limit_bytes=20 << 20),
+        compiler_params=pltpu.CompilerParams(vmem_limit_bytes=28 << 20),
+        cost_estimate=pl.CostEstimate(
+            flops=32 * weights[0].size, bytes_accessed=2 * weights[0].size, transcendentals=0
+        ),
         name="touch",
     )(*weights, *after)
 
@@ -296,7 +306,7 @@
     query_cols = query_weight.shape[1]
     heads = query_cols // dim
     share_blocks = share // block_len
-    late = block_len * max(1, share_blocks // 2)
+    late = max(16, share * 3 // 8 // 16 * 16)
     rest = depth // 4
 
     pieces = [(shift, 0, share) for shift in range(1, groups - 1)]
@@ -338,9 +348,9 @@
 
     own_targets = lax.dynamic_index_in_dim(grid, me, 0, keepdims=False)
 
-    def targets_of(shift, first, length):
-        begin = ((member - shift) % groups) * share_blocks + first // block_len
-        return lax.dynamic_slice_in_dim(own_targets, begin, length // block_len, 0)
+    def targets_of(shift):
+        begin = ((member - shift) % groups) * share_blocks
+        return lax.dynamic_slice_in_dim(own_targets, begin, share_blocks, 0)
 
     weights = (query_weight, keyval_weight)
     slots = (count, block_len)
@@ -350,7 +360,7 @@
     for shift, first, length in pieces[1:-1]:
         early.append(shifted(tokens[first : first + length], shift))
     send_own, own_keyval = project(
-        tokens, weights, "routed", targets=(targets_of(0, 0, share),), slots=slots, fetch=True
+        [tokens], weights, "routed", targets=(targets_of(0),), slots=slots, fetch=True
     )
     shift, first, length = pieces[-1]
     late_most = shifted(tokens[first : first + length, : depth - rest], shift)
@@ -358,14 +368,13 @@
     gathered_own = gather_all(own_keyval, count)
     send_own, gathered_own[1] = lax.optimization_barrier((send_own, gathered_own[1]))
     arrived_own = lax.all_to_all(send_own, "ctx", 0, 0, tiled=True)
-    early_rows = jnp.concatenate(early, axis=0)
-    other_targets = jnp.concatenate([targets_of(*piece) for piece in pieces])
+    other_targets = jnp.concatenate([targets_of(shift) for shift in range(1, groups)])
     touched = touch(weights, gathered_own[1], other_targets)
-    early_query, early_keyval = project(early_rows, weights, "plain", after=(touched,))
+    early_query, early_keyval = project(early, weights, "plain", after=(touched,))
     gathered_early = gather_all(early_keyval, count)
-    sums = project(late_most, weights, "sums")
+    sums = project([late_most], weights, "sums")
     send_other, late_keyval = project(
-        late_rest,
+        [late_rest],
         weights,
         "routed",
         begin=depth - rest,

time: 101 us -> 99 us (0.980)
  other arithmetic: 5.35 us -> 2.53 us
    ppermute x12, waiting for transfers between devices: 11.9 us -> 14.5 us  [gather_all(): pieces.append(lax.ppermute(held, 'ctx', pairs))]
    ppermute x4, waiting for transfers between devices: 26.2 us -> 24.1 us  [shifted(): lax.ppermute(part, 'tp', [(i, (i + shift) % groups) for i in range(groups)])]
    concatenate x9, other arithmetic: 2.41 us -> 0.9 us  [gather_all(): held = pieces[0] if len(pieces) == 1 else jnp.concatenate(pieces, axis=0)]
    concatenate x2 -> x0, other arithmetic: 1.33 us -> none  [the longest x1 1.26 us: step(): early_rows = jnp.concatenate(early, axis=0)]
    ppermute x12, starting transfers between devices: 16.9 us -> 15.6 us  [gather_all(): pieces.append(lax.ppermute(held, 'ctx', pairs))]
    unnamed x10 -> x8, local copies, waits for them, and re-layouts: 5.58 us -> 5.57 us
  transfers between devices with their start and end apart: 18 -> 18, of which waited for: 5 -> 7; matrix products, arithmetic and copies ran while one was open for 8% -> 6% of each run, Pallas kernels for 6% -> 6%
where the time goes in v1:
time: 99 us; the launch traced here: 98.6 us
  waiting for transfers between devices  38.6 us (39%)
  starting transfers between devices  27.5 us (28%)
  Pallas kernels  19.6 us (20%)
  local copies, waits for them, and re-layouts  9.43 us (10%)
  other arithmetic  2.53 us (3%)
    ppermute x4, waiting for transfers between devices, shifted(): lax.ppermute(part, 'tp', [(i, (i + shift) % groups) for i in range(groups)])  24.1 us
    ppermute x12, starting transfers between devices, gather_all(): pieces.append(lax.ppermute(held, 'ctx', pairs))  15.6 us
    ppermute x12, waiting for transfers between devices, gather_all(): pieces.append(lax.ppermute(held, 'ctx', pairs))  14.5 us
    pallas_call x4, Pallas kernels, project(): pl.pallas_call(functools.partial(project_kernel, len(row_parts), begin, b...  13.6 us
    pallas_call x1, Pallas kernels, step(): pl.pallas_call(functools.partial(attend_kernel, count, heads, tuple(segme...  6.07 us
    unnamed x8, local copies, waits for them, and re-layouts  5.57 us
    ppermute x4, starting transfers between devices, shifted(): lax.ppermute(part, 'tp', [(i, (i + shift) % groups) for i in range(groups)])  4.12 us
    all_to_all x1, starting transfers between devices, step(): arrived_own = lax.all_to_all(send_own, 'ctx', 0, 0, tiled=True)  3.92 us
  transfers between devices with their start and end apart: 18, of which 7 were waited for; matrix products, arithmetic and copies ran while one was open for 6% of the time, Pallas kernels for 6%

profile of v1, /device:TPU:0, one launch (start us, length us, event | category | flops | bytes accessed | tf_op | source)
XLA Modules:
  0.0 98.6 jit_solution(17597222218091548645)
XLA Ops:
  0.8 7.6 %shard_map.55 = (bf16[16,32,512]{2,1,0:T(8,128)(2,1)}, bf16[1,128,256]{2,1,0:T(8,128)(2,1)S(1)}) custom-call(s32[4]{0:T(128)S(1)} %get-tuple-element.31.refs_0_, bf16[128,8192]{1,0:T(8,128)(2,1)} %refs_1_.3, bf16[8192,512]{1,0:T(8,128)(2,1)} %refs_2_.7, bf16[8192,256]{1,0:T(8,128)(2,1)} %refs_3_.5), custom_call_target="tpu_custom_call" | custom-call | flops 1610612736 | bytes 14876672 | tf_op jit(solution)/shard_map/pallas_call | solution.py:106
  8.4 4.1 %collective-permute-start = (bf16[1,128,256]{2,1,0:T(8,128)(2,1)S(1)}, bf16[1,128,256]{2,1,0:T(8,128)(2,1)S(1)}, u32[]{:S(2)}, u32[]{:S(2)}) collective-permute-start(bf16[1,128,256]{2,1,0:T(8,128)(2,1)S(1)} %get-tuple-element.16.keyval_refs_0__0_), channel_id=1, source_target_pairs={{0,16},{2,18},{4,20},{6,22},{8,24},{10,26},{12,28},{14,30},{16,0},... | collective-permute-start | bytes 196616 | tf_op jit(solution)/shard_map/ppermute | solution.py:158
  13.2 1.5 %collective-permute-start.1 = (bf16[48,2048]{1,0:T(8,128)(2,1)}, bf16[48,2048]{1,0:T(8,128)(2,1)S(1)}, u32[]{:S(2)}, u32[]{:S(2)}) collective-permute-start(bf16[48,2048]{1,0:T(8,128)(2,1)} %slice.20), channel_id=1, source_target_pairs={{0,1},{1,0},{2,3},{3,2},{4,5},{5,4},{6,7},{7,6},{8,9},{9,8},{10,11... | collective-permute-start | bytes 589832 | tf_op jit(solution)/shard_map/ppermute | solution.py:317
  16.1 1.6 %collective-permute-start.3 = (bf16[16,8192]{1,0:T(8,128)(2,1)S(1)}, bf16[16,8192]{1,0:T(8,128)(2,1)S(1)}, u32[]{:S(2)}, u32[]{:S(2)}) collective-permute-start(bf16[16,8192]{1,0:T(8,128)(2,1)S(1)} %slice.22), channel_id=1, source_target_pairs={{0,1},{1,0},{2,3},{3,2},{4,5},{5,4},{6,7},{7,6},{8,9},{9,8},{10,11... | collective-permute-start | bytes 786440 | tf_op jit(solution)/shard_map/ppermute | solution.py:317
  17.7 1.0 %slice.23 = bf16[64,8192]{1,0:T(8,128)(2,1)} slice(bf16[128,8192]{1,0:T(8,128)(2,1)S(1)} %copy-done.2), slice={[16:80], [0:8192]} | slice | bytes 2097152 | tf_op jit(solution)/shard_map/slice | solution.py:359
  20.0 3.9 %all-to-all-start = ((bf16[16,32,512]{2,1,0:T(8,128)(2,1)}), bf16[16,32,512]{2,1,0:T(8,128)(2,1)S(1)}, u32[]{:S(2)}, u32[]{:S(2)}) async-start(bf16[16,32,512]{2,1,0:T(8,128)(2,1)} %get-tuple-element.17), calls=%async_computation | async-start | bytes 1048576 | tf_op jit(solution)/shard_map/all_to_all | solution.py:370
  25.9 2.0 %collective-permute-start.5 = (bf16[2,128,256]{2,1,0:T(8,128)(2,1)S(1)}, bf16[2,128,256]{2,1,0:T(8,128)(2,1)S(1)}, u32[]{:S(2)}, u32[]{:S(2)}) collective-permute-start(bf16[2,128,256]{2,1,0:T(8,128)(2,1)S(1)} %pad_maximum_fusion.5), channel_id=1, source_target_pairs={{0,4},{2,6},{4,0},{6,2},{8,12},{10,14},{12,8},{14,10},{16,20},{18,... | collective-permute-start | bytes 393224 | tf_op jit(solution)/shard_map/ppermute | solution.py:158
  28.0 3.4 %copy-done = bf16[8192,512]{1,0:T(8,128)(2,1)S(1)} copy-done((bf16[8192,512]{1,0:T(8,128)(2,1)S(1)}, bf16[8192,512]{1,0:T(8,128)(2,1)}, u32[]{:S(2)}) %copy-start) | copy-done | bytes 8388632
  31.4 2.2 %copy-done.1 = bf16[8192,256]{1,0:T(8,128)(2,1)S(1)} copy-done((bf16[8192,256]{1,0:T(8,128)(2,1)S(1)}, bf16[8192,256]{1,0:T(8,128)(2,1)}, u32[]{:S(2)}) %copy-start.1) | copy-done | bytes 4194328
  34.4 2.0 %collective-permute-start.6 = (bf16[4,128,256]{2,1,0:T(8,128)(2,1)}, bf16[4,128,256]{2,1,0:T(8,128)(2,1)S(1)}, u32[]{:S(2)}, u32[]{:S(2)}) collective-permute-start(bf16[4,128,256]{2,1,0:T(8,128)(2,1)} %pad_maximum_fusion.2), channel_id=1, source_target_pairs={{0,8},{2,10},{4,12},{6,14},{8,0},{10,2},{12,4},{14,6},{16,24},{18,... | collective-permute-start | bytes 786440 | tf_op jit(solution)/shard_map/ppermute | solution.py:158
  36.4 3.1 %collective-permute-done.3.refs_0_ = bf16[16,8192]{1,0:T(8,128)(2,1)S(1)} collective-permute-done((bf16[16,8192]{1,0:T(8,128)(2,1)S(1)}, bf16[16,8192]{1,0:T(8,128)(2,1)S(1)}, u32[]{:S(2)}, u32[]{:S(2)}) %collective-permute-start.3) | collective-permute-done | bytes 262176 | tf_op jit(solution)/shard_map/ppermute | solution.py:317
  39.5 21.1 %collective-permute-done.4.refs_1_ = bf16[64,8192]{1,0:T(8,128)(2,1)S(1)} collective-permute-done((bf16[64,8192]{1,0:T(8,128)(2,1)}, bf16[64,8192]{1,0:T(8,128)(2,1)S(1)}, u32[]{:S(2)}, u32[]{:S(2)}) %collective-permute-start.4) | collective-permute-done | bytes 1048608 | tf_op jit(solution)/shard_map/ppermute | solution.py:317
  60.5 2.3 %shard_map.57 = (bf16[80,512]{1,0:T(8,128)(2,1)S(1)}, bf16[1,80,256]{2,1,0:T(8,128)(2,1)S(1)}) custom-call(bf16[16,8192]{1,0:T(8,128)(2,1)S(1)} %collective-permute-done.3.refs_0_, bf16[64,8192]{1,0:T(8,128)(2,1)S(1)} %collective-permute-done.4.refs_1_, bf16[8192,512]{1,0:T(8,128)(2,1)S(1)} %copy-done, bf16[8192,256]{1,0:T(8,128)(2,1)S(1)} %copy-done.1, ...), custom_call_target="tpu_custom_call" | custom-call | flops 1006632960 | bytes 14016512 | tf_op jit(solution)/shard_map/pallas_call | solution.py:106
  63.2 1.7 %shard_map.56 = (f32[48,512]{1,0:T(8,128)S(1)}, f32[48,256]{1,0:T(8,128)S(1)}) custom-call(bf16[48,6144]{1,0:T(8,128)(2,1)S(1)} %collective-permute-done.2.refs_0_, bf16[8192,512]{1,0:T(8,128)(2,1)S(1)} %copy-done, bf16[8192,256]{1,0:T(8,128)(2,1)S(1)} %copy-done.1), custom_call_target="tpu_custom_call" | custom-call | flops 452984832 | bytes 10100736 | tf_op jit(solution)/shard_map/pallas_call | solution.py:106
  64.9 2.0 %shard_map.58 = (bf16[16,32,512]{2,1,0:T(8,128)(2,1)}, bf16[1,48,256]{2,1,0:T(8,128)(2,1)S(1)}) custom-call(s32[4]{0:T(128)S(1)} %get-tuple-element.30.refs_3_.refs_0_, bf16[48,2048]{1,0:T(8,128)(2,1)S(1)} %collective-permute-done.1.refs_1_, bf16[8192,512]{1,0:T(8,128)(2,1)S(1)} %copy-done, bf16[8192,256]{1,0:T(8,128)(2,1)S(1)} %copy-done.1, ...), custom_call_target="tpu_custom_call" | custom-call | flops 150994944 | bytes 3416064 | tf_op jit(solution)/shard_map/pallas_call | solution.py:106
  66.9 2.6 %collective-permute-start.12 = (bf16[1,48,256]{2,1,0:T(8,128)(2,1)S(1)}, bf16[1,48,256]{2,1,0:T(8,128)(2,1)S(1)}, u32[]{:S(2)}, u32[]{:S(2)}) collective-permute-start(bf16[1,48,256]{2,1,0:T(8,128)(2,1)S(1)} %get-tuple-element.24.keyval_refs_2__0_), channel_id=1, source_target_pairs={{0,16},{2,18},{4,20},{6,22},{8,24},{10,26},{12,28},{14,30},{16,0},... | collective-permute-start | bytes 73736 | tf_op jit(solution)/shard_map/ppermute | solution.py:158
  69.5 3.9 %all-to-all-start.1 = ((bf16[16,32,512]{2,1,0:T(8,128)(2,1)}), bf16[16,32,512]{2,1,0:T(8,128)(2,1)S(1)}, u32[]{:S(2)}, u32[]{:S(2)}) async-start(bf16[16,32,512]{2,1,0:T(8,128)(2,1)} %get-tuple-element.22), calls=%async_computation.1 | async-start | bytes 1048576 | tf_op jit(solution)/shard_map/all_to_all | solution.py:387
  73.5 2.0 %collective-permute-start.9 = (bf16[2,80,256]{2,1,0:T(8,128)(2,1)S(1)}, bf16[2,80,256]{2,1,0:T(8,128)(2,1)S(1)}, u32[]{:S(2)}, u32[]{:S(2)}) collective-permute-start(bf16[2,80,256]{2,1,0:T(8,128)(2,1)S(1)} %pad_maximum_fusion.7), channel_id=1, source_target_pairs={{0,4},{2,6},{4,0},{6,2},{8,12},{10,14},{12,8},{14,10},{16,20},{18,... | collective-permute-start | bytes 245768 | tf_op jit(solution)/shard_map/ppermute | solution.py:158
  75.7 6.7 %collective-permute-done.9.keyval_refs_1__2_ = bf16[2,80,256]{2,1,0:T(8,128)(2,1)S(1)} collective-permute-done((bf16[2,80,256]{2,1,0:T(8,128)(2,1)S(1)}, bf16[2,80,256]{2,1,0:T(8,128)(2,1)S(1)}, u32[]{:S(2)}, u32[]{:S(2)}) %collective-permute-start.9) | collective-permute-done | bytes 81952 | tf_op jit(solution)/shard_map/ppermute | solution.py:158
  82.4 1.2 %collective-permute-start.10 = (bf16[4,80,256]{2,1,0:T(8,128)(2,1)S(1)}, bf16[4,80,256]{2,1,0:T(8,128)(2,1)S(1)}, u32[]{:S(2)}, u32[]{:S(2)}) collective-permute-start(bf16[4,80,256]{2,1,0:T(8,128)(2,1)S(1)} %pad_maximum_fusion.4), channel_id=1, source_target_pairs={{0,8},{2,10},{4,12},{6,14},{8,0},{10,2},{12,4},{14,6},{16,24},{18,... | collective-permute-start | bytes 491528 | tf_op jit(solution)/shard_map/ppermute | solution.py:158
  83.8 0.9 collective-permute-start.14
  84.8 5.2 %collective-permute-done.10.keyval_refs_1__3_ = bf16[4,80,256]{2,1,0:T(8,128)(2,1)S(1)} collective-permute-done((bf16[4,80,256]{2,1,0:T(8,128)(2,1)S(1)}, bf16[4,80,256]{2,1,0:T(8,128)(2,1)S(1)}, u32[]{:S(2)}, u32[]{:S(2)}) %collective-permute-start.10) | collective-permute-done | bytes 163872 | tf_op jit(solution)/shard_map/ppermute | solution.py:158
  91.2 1.4 %collective-permute-done.15.keyval_refs_2__4_ = bf16[8,48,256]{2,1,0:T(8,128)(2,1)S(1)} collective-permute-done((bf16[8,48,256]{2,1,0:T(8,128)(2,1)S(1)}, bf16[8,48,256]{2,1,0:T(8,128)(2,1)S(1)}, u32[]{:S(2)}, u32[]{:S(2)}) %collective-permute-start.15) | collective-permute-done | bytes 196640 | tf_op jit(solution)/shard_map/ppermute | solution.py:158
  92.6 6.1 %attend.1 = bf16[256,512]{1,0:T(8,128)(2,1)} custom-call(s32[5]{0:T(128)S(1)} %stack.23.info_ref, s32[8]{0:T(128)S(1)} %select_reduce_fusion.4.source_ref, s32[8]{0:T(128)S(1)} %convert_reduce_fusion.rank_ref, s32[136]{0:T(256)S(1)} %broadcast_subtract_fusion.item_block_ref, s32[136]{0:T(256)S(1)} %get-tuple-element.25.item_tile_ref, ...), custom_call_target="tpu_custom_call" | custom-call | tf_op jit(solution)/shard_map/attend/pallas_call | solution.py:401
  (59 shorter events, 8.3 us)
Async XLA Ops:
  0.8 11.7 %copy-start.2 = (bf16[128,8192]{1,0:T(8,128)(2,1)S(1)}, bf16[128,8192]{1,0:T(8,128)(2,1)}, u32[]{:S(2)}) copy-start(bf16[128,8192]{1,0:T(8,128)(2,1)} %refs_1_.3) | copy-start | bytes 6291460
  8.4 11.0 %copy-start.3 = (s32[32]{0:T(128)S(1)}, s32[32]{0:T(128)}, u32[]{:S(2)}) copy-start(s32[32]{0:T(128)} %param.8) | copy-start | bytes 388
  8.4 11.6 %collective-permute-start = (bf16[1,128,256]{2,1,0:T(8,128)(2,1)S(1)}, bf16[1,128,256]{2,1,0:T(8,128)(2,1)S(1)}, u32[]{:S(2)}, u32[]{:S(2)}) collective-permute-start(bf16[1,128,256]{2,1,0:T(8,128)(2,1)S(1)} %get-tuple-element.16.keyval_refs_0__0_), channel_id=1, source_target_pairs={{0,16},{2,18},{4,20},{6,22},{8,24},{10,26},{12,28},{14,30},{16,0},... | collective-permute-start | bytes 196616 | tf_op jit(solution)/shard_map/ppermute | solution.py:158
  13.2 51.7 %collective-permute-start.1 = (bf16[48,2048]{1,0:T(8,128)(2,1)}, bf16[48,2048]{1,0:T(8,128)(2,1)S(1)}, u32[]{:S(2)}, u32[]{:S(2)}) collective-permute-start(bf16[48,2048]{1,0:T(8,128)(2,1)} %slice.20), channel_id=1, source_target_pairs={{0,1},{1,0},{2,3},{3,2},{4,5},{5,4},{6,7},{7,6},{8,9},{9,8},{10,11... | collective-permute-start | bytes 589832 | tf_op jit(solution)/shard_map/ppermute | solution.py:317
  15.6 47.6 %collective-permute-start.2 = (bf16[48,6144]{1,0:T(8,128)(2,1)}, bf16[48,6144]{1,0:T(8,128)(2,1)S(1)}, u32[]{:S(2)}, u32[]{:S(2)}) collective-permute-start(bf16[48,6144]{1,0:T(8,128)(2,1)} %slice.21), channel_id=1, source_target_pairs={{0,1},{1,0},{2,3},{3,2},{4,5},{5,4},{6,7},{7,6},{8,9},{9,8},{10,11... | collective-permute-start | bytes 1769480 | tf_op jit(solution)/shard_map/ppermute | solution.py:317
  16.1 23.3 %collective-permute-start.3 = (bf16[16,8192]{1,0:T(8,128)(2,1)S(1)}, bf16[16,8192]{1,0:T(8,128)(2,1)S(1)}, u32[]{:S(2)}, u32[]{:S(2)}) collective-permute-start(bf16[16,8192]{1,0:T(8,128)(2,1)S(1)} %slice.22), channel_id=1, source_target_pairs={{0,1},{1,0},{2,3},{3,2},{4,5},{5,4},{6,7},{7,6},{8,9},{9,8},{10,11... | collective-permute-start | bytes 786440 | tf_op jit(solution)/shard_map/ppermute | solution.py:317
  18.7 41.8 %collective-permute-start.4 = (bf16[64,8192]{1,0:T(8,128)(2,1)}, bf16[64,8192]{1,0:T(8,128)(2,1)S(1)}, u32[]{:S(2)}, u32[]{:S(2)}) collective-permute-start(bf16[64,8192]{1,0:T(8,128)(2,1)} %slice.23), channel_id=1, source_target_pairs={{0,1},{1,0},{2,3},{3,2},{4,5},{5,4},{6,7},{7,6},{8,9},{9,8},{10,11... | collective-permute-start | bytes 3145736 | tf_op jit(solution)/shard_map/ppermute | solution.py:317
  20.0 49.6 %all-to-all-start = ((bf16[16,32,512]{2,1,0:T(8,128)(2,1)}), bf16[16,32,512]{2,1,0:T(8,128)(2,1)S(1)}, u32[]{:S(2)}, u32[]{:S(2)}) async-start(bf16[16,32,512]{2,1,0:T(8,128)(2,1)} %get-tuple-element.17), calls=%async_computation | async-start | bytes 1048576 | tf_op jit(solution)/shard_map/all_to_all | solution.py:370
  25.9 7.8 %collective-permute-start.5 = (bf16[2,128,256]{2,1,0:T(8,128)(2,1)S(1)}, bf16[2,128,256]{2,1,0:T(8,128)(2,1)S(1)}, u32[]{:S(2)}, u32[]{:S(2)}) collective-permute-start(bf16[2,128,256]{2,1,0:T(8,128)(2,1)S(1)} %pad_maximum_fusion.5), channel_id=1, source_target_pairs={{0,4},{2,6},{4,0},{6,2},{8,12},{10,14},{12,8},{14,10},{16,20},{18,... | collective-permute-start | bytes 393224 | tf_op jit(solution)/shard_map/ppermute | solution.py:158
  28.0 3.4 %copy-start = (bf16[8192,512]{1,0:T(8,128)(2,1)S(1)}, bf16[8192,512]{1,0:T(8,128)(2,1)}, u32[]{:S(2)}) copy-start(bf16[8192,512]{1,0:T(8,128)(2,1)} %refs_2_.7) | copy-start | bytes 25165828
  31.4 2.2 %copy-start.1 = (bf16[8192,256]{1,0:T(8,128)(2,1)S(1)}, bf16[8192,256]{1,0:T(8,128)(2,1)}, u32[]{:S(2)}) copy-start(bf16[8192,256]{1,0:T(8,128)(2,1)} %refs_3_.5) | copy-start | bytes 12582916
  34.4 49.2 %collective-permute-start.6 = (bf16[4,128,256]{2,1,0:T(8,128)(2,1)}, bf16[4,128,256]{2,1,0:T(8,128)(2,1)S(1)}, u32[]{:S(2)}, u32[]{:S(2)}) collective-permute-start(bf16[4,128,256]{2,1,0:T(8,128)(2,1)} %pad_maximum_fusion.2), channel_id=1, source_target_pairs={{0,8},{2,10},{4,12},{6,14},{8,0},{10,2},{12,4},{14,6},{16,24},{18,... | collective-permute-start | bytes 786440 | tf_op jit(solution)/shard_map/ppermute | solution.py:158
  62.8 10.7 %collective-permute-start.8 = (bf16[1,80,256]{2,1,0:T(8,128)(2,1)S(1)}, bf16[1,80,256]{2,1,0:T(8,128)(2,1)S(1)}, u32[]{:S(2)}, u32[]{:S(2)}) collective-permute-start(bf16[1,80,256]{2,1,0:T(8,128)(2,1)S(1)} %get-tuple-element.23.keyval_refs_1__0_), channel_id=1, source_target_pairs={{0,16},{2,18},{4,20},{6,22},{8,24},{10,26},{12,28},{14,30},{16,0},... | collective-permute-start | bytes 122888 | tf_op jit(solution)/shard_map/ppermute | solution.py:158
  66.9 8.6 %collective-permute-start.12 = (bf16[1,48,256]{2,1,0:T(8,128)(2,1)S(1)}, bf16[1,48,256]{2,1,0:T(8,128)(2,1)S(1)}, u32[]{:S(2)}, u32[]{:S(2)}) collective-permute-start(bf16[1,48,256]{2,1,0:T(8,128)(2,1)S(1)} %get-tuple-element.24.keyval_refs_2__0_), channel_id=1, source_target_pairs={{0,16},{2,18},{4,20},{6,22},{8,24},{10,26},{12,28},{14,30},{16,0},... | collective-permute-start | bytes 73736 | tf_op jit(solution)/shard_map/ppermute | solution.py:158
  69.5 23.0 %all-to-all-start.1 = ((bf16[16,32,512]{2,1,0:T(8,128)(2,1)}), bf16[16,32,512]{2,1,0:T(8,128)(2,1)S(1)}, u32[]{:S(2)}, u32[]{:S(2)}) async-start(bf16[16,32,512]{2,1,0:T(8,128)(2,1)} %get-tuple-element.22), calls=%async_computation.1 | async-start | bytes 1048576 | tf_op jit(solution)/shard_map/all_to_all | solution.py:387
  73.5 8.9 %collective-permute-start.9 = (bf16[2,80,256]{2,1,0:T(8,128)(2,1)S(1)}, bf16[2,80,256]{2,1,0:T(8,128)(2,1)S(1)}, u32[]{:S(2)}, u32[]{:S(2)}) collective-permute-start(bf16[2,80,256]{2,1,0:T(8,128)(2,1)S(1)} %pad_maximum_fusion.7), channel_id=1, source_target_pairs={{0,4},{2,6},{4,0},{6,2},{8,12},{10,14},{12,8},{14,10},{16,20},{18,... | collective-permute-start | bytes 245768 | tf_op jit(solution)/shard_map/ppermute | solution.py:158
  75.5 8.3 %collective-permute-start.13 = (bf16[2,48,256]{2,1,0:T(8,128)(2,1)S(1)}, bf16[2,48,256]{2,1,0:T(8,128)(2,1)S(1)}, u32[]{:S(2)}, u32[]{:S(2)}) collective-permute-start(bf16[2,48,256]{2,1,0:T(8,128)(2,1)S(1)} %pad_maximum_fusion.8), channel_id=1, source_target_pairs={{0,4},{2,6},{4,0},{6,2},{8,12},{10,14},{12,8},{14,10},{16,20},{18,... | collective-permute-start | bytes 147464 | tf_op jit(solution)/shard_map/ppermute | solution.py:158
  82.4 7.6 %collective-permute-start.10 = (bf16[4,80,256]{2,1,0:T(8,128)(2,1)S(1)}, bf16[4,80,256]{2,1,0:T(8,128)(2,1)S(1)}, u32[]{:S(2)}, u32[]{:S(2)}) collective-permute-start(bf16[4,80,256]{2,1,0:T(8,128)(2,1)S(1)} %pad_maximum_fusion.4), channel_id=1, source_target_pairs={{0,8},{2,10},{4,12},{6,14},{8,0},{10,2},{12,4},{14,6},{16,24},{18,... | collective-permute-start | bytes 491528 | tf_op jit(solution)/shard_map/ppermute | solution.py:158
  83.7 7.5 %collective-permute-start.7 = (bf16[8,128,256]{2,1,0:T(8,128)(2,1)S(1)}, bf16[8,128,256]{2,1,0:T(8,128)(2,1)S(1)}, u32[]{:S(2)}, u32[]{:S(2)}) collective-permute-start(bf16[8,128,256]{2,1,0:T(8,128)(2,1)S(1)} %pad_maximum_fusion), channel_id=1, source_target_pairs={{0,2},{2,0},{4,6},{6,4},{8,10},{10,8},{12,14},{14,12},{16,18},{18,... | collective-permute-start | bytes 1572872 | tf_op jit(solution)/shard_map/ppermute | solution.py:158
  83.8 7.2 %collective-permute-start.14 = (bf16[4,48,256]{2,1,0:T(8,128)(2,1)S(1)}, bf16[4,48,256]{2,1,0:T(8,128)(2,1)S(1)}, u32[]{:S(2)}, u32[]{:S(2)}) collective-permute-start(bf16[4,48,256]{2,1,0:T(8,128)(2,1)S(1)} %pad_maximum_fusion.6), channel_id=1, source_target_pairs={{0,8},{2,10},{4,12},{6,14},{8,0},{10,2},{12,4},{14,6},{16,24},{18,... | collective-permute-start | bytes 294920 | tf_op jit(solution)/shard_map/ppermute | solution.py:158
  90.0 2.6 %collective-permute-start.11 = (bf16[8,80,256]{2,1,0:T(8,128)(2,1)S(1)}, bf16[8,80,256]{2,1,0:T(8,128)(2,1)S(1)}, u32[]{:S(2)}, u32[]{:S(2)}) collective-permute-start(bf16[8,80,256]{2,1,0:T(8,128)(2,1)S(1)} %pad_maximum_fusion.1), channel_id=1, source_target_pairs={{0,2},{2,0},{4,6},{6,4},{8,10},{10,8},{12,14},{14,12},{16,18},{18,... | collective-permute-start | bytes 983048 | tf_op jit(solution)/shard_map/ppermute | solution.py:158
  91.1 1.5 %collective-permute-start.15 = (bf16[8,48,256]{2,1,0:T(8,128)(2,1)S(1)}, bf16[8,48,256]{2,1,0:T(8,128)(2,1)S(1)}, u32[]{:S(2)}, u32[]{:S(2)}) collective-permute-start(bf16[8,48,256]{2,1,0:T(8,128)(2,1)S(1)} %pad_maximum_fusion.3), channel_id=1, source_target_pairs={{0,2},{2,0},{4,6},{6,4},{8,10},{10,8},{12,14},{14,12},{16,18},{18,... | collective-permute-start | bytes 589832 | tf_op jit(solution)/shard_map/ppermute | solution.py:158

commit v2 on v1

--- a/solution.py
+++ b/solution.py
@@ -26,51 +26,20 @@
             first, row = first + length, row + length
 
 
-def fetched_product(rows_ref, weights, stages, accs, sems):
-    chunks = sems.shape[0]
-    step = rows_ref.shape[1] // chunks
-
-    def fetches(chunk):
-        at = pl.ds(chunk * step, step)
-        return [
-            pltpu.make_async_copy(weight.at[at], stage.at[at], sems.at[chunk, k])
-            for k, (weight, stage) in enumerate(zip(weights, stages))
-        ]
-
-    for chunk in range(chunks):
-        for fetch in fetches(chunk):
-            fetch.start()
-    for chunk in range(chunks):
-        for fetch in fetches(chunk):
-            fetch.wait()
-        at = slice(chunk * step, (chunk + 1) * step)
-        for stage, acc in zip(stages, accs):
-            product = jnp.dot(rows_ref[:, at], stage[at], preferred_element_type=jnp.float32)
-            if chunk > 0:
-                acc[...] += product
-            else:
-                acc[...] = product
-    return [acc[...] for acc in accs]
-
-
-def project_kernel(parts, begin, carried, held, kind, fetch, after, *refs):
+def project_kernel(parts, begin, carried, held, kind, after, *refs):
     refs = list(refs)
     target_ref = refs.pop(0) if kind == "routed" else None
     row_refs = [refs.pop(0) for _ in range(parts)]
     weights = [refs.pop(0), refs.pop(0)]
     given = [refs.pop(0), refs.pop(0)] if carried else None
-    held_ref = refs.pop(0) if held else None
+    held_refs = [refs.pop(0) for _ in range(held)]
     refs = refs[after:]
     outs = [refs.pop(0), refs.pop(0)]
-    if fetch:
-        sums = fetched_product(row_refs[0], weights, refs[:2], refs[2:4], refs[4])
-    else:
-        rows = jnp.concatenate([ref[...] for ref in row_refs], axis=0)
-        at = slice(begin, begin + rows.shape[1])
-        sums = [
-            jnp.dot(rows, weight[at], preferred_element_type=jnp.float32)
-            for weight in weights
-        ]
+    rows = jnp.concatenate([ref[...] for ref in row_refs], axis=0)
+    at = slice(begin, begin + rows.shape[1])
+    sums = [
+        jnp.dot(rows, weight[at], preferred_element_type=jnp.float32) for weight in weights
+    ]
     if carried:
         sums = [ref[...] + product for ref, product in zip(given, sums)]
     if kind == "sums":
@@ -79,13 +48,13 @@
         return
     query, keyval = (product.astype(jnp.bfloat16) for product in sums)
     if kind == "routed":
-        route(([held_ref[...]] if held else []) + [query], target_ref, outs[0])
+        route([ref[...] for ref in held_refs] + [query], target_ref, outs[0])
     else:
         outs[0][...] = query
     outs[1][0] = keyval
 
 
-def project(row_parts, weights, kind, begin=0, given=(), held=(), targets=(), slots=None, fetch=False, after=()):
+def project(row_parts, weights, kind, begin=0, given=(), held=(), targets=(), slots=None, after=()):
     length, depth = sum(rows.shape[0] for rows in row_parts), row_parts[0].shape[1]
     widths = [weight.shape[1] for weight in weights]
     columns = sum(widths)
@@ -97,52 +66,24 @@
         shapes = [
             jax.ShapeDtypeStruct(shape, jnp.bfloat16) for shape in (first, (1, length, widths[1]))
         ]
-    scratch = []
-    if fetch:
-        scratch = [pltpu.VMEM((depth, width), jnp.bfloat16) for width in widths]
-        scratch += [pltpu.VMEM((length, width), jnp.float32) for width in widths]
-        scratch += [pltpu.SemaphoreType.DMA((math.gcd(depth // 256, 8), 2))]
-    weight_spec = pl.BlockSpec(memory_space=pl.ANY) if fetch else vmem
     return pl.pallas_call(
         functools.partial(
-            project_kernel, len(row_parts), begin, bool(given), bool(held), kind, fetch, len(after)
+            project_kernel, len(row_parts), begin, bool(given), len(held), kind, len(after)
         ),
         out_shape=shapes,
         in_specs=[pl.BlockSpec(memory_space=pltpu.SMEM)] * len(targets)
         + [vmem] * len(row_parts)
-        + [weight_spec] * 2
+        + [vmem] * 2
         + [vmem] * (len(given) + len(held))
         + [pl.BlockSpec(memory_space=pl.ANY)] * len(after),
         out_specs=[vmem] * len(shapes),
-        scratch_shapes=scratch,
-        compiler_params=pltpu.CompilerParams(vmem_limit_bytes=(52 if fetch else 28) << 20),
+        compiler_params=pltpu.CompilerParams(vmem_limit_bytes=28 << 20),
         cost_estimate=pl.CostEstimate(
             flops=2 * length * depth * columns,
             bytes_accessed=2 * (length * depth + depth * columns + length * columns),
             transcendentals=0,
         ),
     )(*targets, *row_parts, *weights, *given, *held, *after)
-
-
-def touch_kernel(*refs):
-    ref, out_ref = refs[0], refs[-1]
-    out_ref[...] = ref[: out_ref.shape[0], : out_ref.shape[1]]
-
-
-def touch(weights, *after):
-    vmem = pl.BlockSpec(memory_space=pltpu.VMEM)
-    hbm = pl.BlockSpec(memory_space=pl.ANY)
-    return pl.pallas_call(
-        touch_kernel,
-        out_shape=jax.ShapeDtypeStruct((16, 128), weights[0].dtype),
-        in_specs=[vmem] * len(weights) + [hbm] * len(after),
-        out_specs=vmem,
-        compiler_params=pltpu.CompilerParams(vmem_limit_bytes=28 << 20),
-        cost_estimate=pl.CostEstimate(
-            flops=32 * weights[0].size, bytes_accessed=2 * weights[0].size, transcendentals=0
-        ),
-        name="touch",
-    )(*weights, *after)
 
 
 def gather_bits(count):
@@ -182,7 +123,7 @@
     item_tile_ref,
     start_ref,
     place_ref,
-    arrived_refs,
+    arrived_ref,
     keyval_refs,
     out_ref,
     key_ref,
@@ -194,13 +135,11 @@
     acc_ref,
 ):
     blocks, per_block = start_ref.shape
-    block_len = arrived_refs[0].shape[1]
+    block_len = arrived_ref.shape[1]
     dim = key_ref.shape[2]
     rows = key_ref.shape[1]
     me = info_ref[0]
     iterations = info_ref[1]
-    own_place = info_ref[2]
-    own_blocks = keyval_refs[0][0].shape[1] // block_len
 
     def place_rows(slots, piece_of, offset_at, first, length):
         row = pl.multiple_of(info_ref[offset_at] + first, 16)
@@ -222,21 +161,10 @@
         valt_ref[tile] = value_ref[tile].T
 
     for block in range(blocks):
-        own = (block >= own_place) & (block < own_place + own_blocks)
-
-        def take(ref, index):
-            for head in range(heads):
-                query_ref[block, head * block_len : (head + 1) * block_len, :] = ref[
-                    index, :, head * dim : (head + 1) * dim
-                ]
-
-        @pl.when(own)
-        def _():
-            take(arrived_refs[0], source_ref[block])
-
-        @pl.when(jnp.logical_not(own))
-        def _():
-            take(arrived_refs[1], source_ref[block])
+        for head in range(heads):
+            query_ref[block, head * block_len : (head + 1) * block_len, :] = arrived_ref[
+                source_ref[block], :, head * dim : (head + 1) * dim
+            ]
 
     max_ref[...] = jnp.full_like(max_ref, NEG_FILL)
     sum_ref[...] = jnp.zeros_like(sum_ref)
@@ -260,7 +188,7 @@
             base = tile * rows
             start = start_ref[pl.ds(safe, 1), :] - base
             place = place_ref[pl.ds(safe, 1), :] - base
-            allowed = (key_index >= start) & (key_index <= place)
+            allowed = (key_index - start).astype(jnp.uint32) <= (place - start).astype(jnp.uint32)
             scores = jnp.where(allowed, scores * scale, NEG_FILL)
             highest = jnp.max(scores, axis=0, keepdims=True)
             weights = jnp.exp2(scores - highest)
@@ -352,6 +280,12 @@
         begin = ((member - shift) % groups) * share_blocks
         return lax.dynamic_slice_in_dim(own_targets, begin, share_blocks, 0)
 
+    offsets = [((member - shift) % groups) * share for shift in range(groups)]
+    info = jnp.stack([me, iterations, *offsets]).astype(jnp.int32)
+    starts = jnp.tile(row_start, (1, heads))
+    places = jnp.tile(row_place, (1, heads))
+    targets = jnp.concatenate([targets_of(shift) for shift in range(groups)])
+    integers = (info, sources, rank, item_block, item_tile, starts, places, targets)
     weights = (query_weight, keyval_weight)
     slots = (count, block_len)
     shift, first, length = pieces[0]
@@ -359,49 +293,41 @@
     early.append(shifted(tokens[first + head : first + length], shift))
     for shift, first, length in pieces[1:-1]:
         early.append(shifted(tokens[first : first + length], shift))
-    send_own, own_keyval = project(
-        [tokens], weights, "routed", targets=(targets_of(0),), slots=slots, fetch=True
-    )
+    own_query, own_keyval = project([tokens], weights, "plain", after=integers)
     shift, first, length = pieces[-1]
     late_most = shifted(tokens[first : first + length, : depth - rest], shift)
     late_rest = shifted(tokens[first : first + length, depth - rest :], shift)
     gathered_own = gather_all(own_keyval, count)
-    send_own, gathered_own[1] = lax.optimization_barrier((send_own, gathered_own[1]))
-    arrived_own = lax.all_to_all(send_own, "ctx", 0, 0, tiled=True)
-    other_targets = jnp.concatenate([targets_of(shift) for shift in range(1, groups)])
-    touched = touch(weights, gathered_own[1], other_targets)
-    early_query, early_keyval = project(early, weights, "plain", after=(touched,))
+    early_query, early_keyval = project(early, weights, "plain")
     gathered_early = gather_all(early_keyval, count)
     sums = project([late_most], weights, "sums")
-    send_other, late_keyval = project(
+    send, late_keyval = project(
         [late_rest],
         weights,
         "routed",
         begin=depth - rest,
         given=sums,
-        held=(early_query,),
-        targets=(other_targets,),
+        held=(own_query, early_query),
+        targets=(targets,),
         slots=slots,
     )
     gathered_late = gather_all(late_keyval, count)
-    arrived_other = lax.all_to_all(send_other, "ctx", 0, 0, tiled=True)
-
-    segments = [(0, 0, 3, 0, share)]
+    arrived = lax.all_to_all(send, "ctx", 0, 0, tiled=True)
+
+    segments = [(0, 0, 2, 0, share)]
     begin = 0
     for shift, first, length in pieces[:-1]:
-        segments.append((1, begin, 3 + shift, first, length))
+        segments.append((1, begin, 2 + shift, first, length))
         begin += length
-    segments.append((2, 0, 3 + pieces[-1][0], pieces[-1][1], late))
-    offsets = [((member - shift) % groups) * share for shift in range(groups)]
-
-    info = jnp.stack([me, iterations, member * share_blocks, *offsets]).astype(jnp.int32)
+    segments.append((2, 0, 2 + pieces[-1][0], pieces[-1][1], late))
+
     per_block = heads * block_len
     smem = pl.BlockSpec(memory_space=pltpu.SMEM)
     vmem = pl.BlockSpec(memory_space=pltpu.VMEM)
     return pl.pallas_call(
         functools.partial(attend_kernel, count, heads, tuple(segments)),
         out_shape=jax.ShapeDtypeStruct((rows, query_cols), jnp.bfloat16),
-        in_specs=[smem] * 5 + [vmem] * 2 + [[vmem] * 2, [[vmem] * len(gathered_late)] * 3],
+        in_specs=[smem] * 5 + [vmem] * 2 + [vmem, [[vmem] * len(gathered_late)] * 3],
         out_specs=vmem,
         scratch_shapes=[
             pltpu.VMEM((count, rows, dim), jnp.bfloat16),
@@ -420,9 +346,9 @@
         rank,
         item_block,
         item_tile,
-        jnp.tile(row_start, (1, heads)),
-        jnp.tile(row_place, (1, heads)),
-        [arrived_own, arrived_other],
+        starts,
+        places,
+        arrived,
         [gathered_own, gathered_early, gathered_late],
     )
 

time: 99 us -> 94.7 us (0.957)
  Pallas kernels: 19.6 us -> 14.6 us
  starting transfers between devices: 27.5 us -> 25.7 us
  local copies, waits for them, and re-layouts: 9.43 us -> 11.1 us
    ppermute x12, waiting for transfers between devices: 14.5 us -> 23.3 us  [gather_all(): pieces.append(lax.ppermute(held, 'ctx', pairs))]
    ppermute x4, waiting for transfers between devices: 24.1 us -> 16 us  [shifted(): lax.ppermute(part, 'tp', [(i, (i + shift) % groups) for i in range(groups)])]
    pallas_call x4, Pallas kernels: 13.6 us -> 8.88 us  [project(): pl.pallas_call(functools.partial(project_kernel, len(row_parts), begin, b...]
    all_to_all x2 -> x1, starting transfers between devices: 7.84 us -> 3.91 us  [step(): arrived = lax.all_to_all(send, 'ctx', 0, 0, tiled=True)]
    ppermute x4, starting transfers between devices: 4.12 us -> 6.09 us  [shifted(): lax.ppermute(part, 'tp', [(i, (i + shift) % groups) for i in range(groups)])]
    slice x1, local copies, waits for them, and re-layouts: 1.03 us -> 2.26 us  [step(): early.append(shifted(tokens[first + head:first + length], shift))]
    slice x1, local copies, waits for them, and re-layouts: 0.87 us -> 2.08 us  [step(): late_most = shifted(tokens[first:first + length, :depth - rest], shift)]
    unnamed x8 -> x10, local copies, waits for them, and re-layouts: 5.57 us -> 5.58 us
  transfers between devices with their start and end apart: 18 -> 17, of which waited for: 7 -> 8; matrix products, arithmetic and copies ran while one was open for 6% -> 6% of each run, Pallas kernels for 6% -> 9%
where the time goes in v2:
time: 94.7 us; the launch traced here: 94.3 us
  waiting for transfers between devices  39.3 us (41%)
  starting transfers between devices  25.7 us (27%)
  Pallas kernels  14.6 us (15%)
  local copies, waits for them, and re-layouts  11.1 us (12%)
  other arithmetic  2.58 us (3%)
  between operations  0.95 us (1%)
    ppermute x12, waiting for transfers between devices, gather_all(): pieces.append(lax.ppermute(held, 'ctx', pairs))  23.3 us
    ppermute x4, waiting for transfers between devices, shifted(): lax.ppermute(part, 'tp', [(i, (i + shift) % groups) for i in range(groups)])  16 us
    ppermute x12, starting transfers between devices, gather_all(): pieces.append(lax.ppermute(held, 'ctx', pairs))  15.8 us
    pallas_call x4, Pallas kernels, project(): pl.pallas_call(functools.partial(project_kernel, len(row_parts), begin, b...  8.88 us
    ppermute x4, starting transfers between devices, shifted(): lax.ppermute(part, 'tp', [(i, (i + shift) % groups) for i in range(groups)])  6.09 us
    pallas_call x1, Pallas kernels, step(): pl.pallas_call(functools.partial(attend_kernel, count, heads, tuple(segme...  5.68 us
    unnamed x10, local copies, waits for them, and re-layouts  5.58 us
    all_to_all x1, starting transfers between devices, step(): arrived = lax.all_to_all(send, 'ctx', 0, 0, tiled=True)  3.91 us
  transfers between devices with their start and end apart: 17, of which 8 were waited for; matrix products, arithmetic and copies ran while one was open for 6% of the time, Pallas kernels for 9%

profile of v2, /device:TPU:0, one launch (start us, length us, event | category | flops | bytes accessed | tf_op | source)
XLA Modules:
  0.0 94.3 jit_solution(15318592868180445531)
XLA Ops:
  0.0 2.1 %slice.21 = bf16[48,6144]{1,0:T(8,128)(2,1)} slice(bf16[128,8192]{1,0:T(8,128)(2,1)} %refs_0_.1), slice={[80:128], [0:6144]} | slice | bytes 1179648 | tf_op jit(solution)/shard_map/slice | solution.py:298
  2.1 3.0 %collective-permute-start.1 = (bf16[48,6144]{1,0:T(8,128)(2,1)}, bf16[48,6144]{1,0:T(8,128)(2,1)}, u32[]{:S(2)}, u32[]{:S(2)}) collective-permute-start(bf16[48,6144]{1,0:T(8,128)(2,1)} %slice.21), channel_id=1, source_target_pairs={{0,1},{1,0},{2,3},{3,2},{4,5},{5,4},{6,7},{7,6},{8,9},{9,8},{10,11... | collective-permute-start | bytes 1769480 | tf_op jit(solution)/shard_map/ppermute | solution.py:245
  5.0 2.3 %slice.23 = bf16[64,8192]{1,0:T(8,128)(2,1)} slice(bf16[128,8192]{1,0:T(8,128)(2,1)} %refs_0_.1), slice={[16:80], [0:8192]} | slice | bytes 2097152 | tf_op jit(solution)/shard_map/slice | solution.py:293
  11.6 3.4 %copy-done = bf16[8192,512]{1,0:T(8,128)(2,1)S(1)} copy-done((bf16[8192,512]{1,0:T(8,128)(2,1)S(1)}, bf16[8192,512]{1,0:T(8,128)(2,1)}, u32[]{:S(2)}) %copy-start) | copy-done | bytes 8388632
  15.0 2.2 %copy-done.1 = bf16[8192,256]{1,0:T(8,128)(2,1)S(1)} copy-done((bf16[8192,256]{1,0:T(8,128)(2,1)S(1)}, bf16[8192,256]{1,0:T(8,128)(2,1)}, u32[]{:S(2)}) %copy-start.1) | copy-done | bytes 4194328
  17.2 1.8 %shard_map.56 = (bf16[128,512]{1,0:T(8,128)(2,1)S(1)}, bf16[1,128,256]{2,1,0:T(8,128)(2,1)S(1)}) custom-call(bf16[128,8192]{1,0:T(8,128)(2,1)S(1)} %copy-done.2, bf16[8192,512]{1,0:T(8,128)(2,1)S(1)} %copy-done, bf16[8192,256]{1,0:T(8,128)(2,1)S(1)} %copy-done.1, s32[4]{0:T(128)S(1)} %pad_add_fusion.refs_3_.info_ref, ...), custom_call_target="tpu_custom_call" | custom-call | flops 1610612736 | bytes 14876672 | tf_op jit(solution)/shard_map/pallas_call | solution.py:69
  19.0 3.2 %collective-permute-start.4 = (bf16[1,128,256]{2,1,0:T(8,128)(2,1)S(1)}, bf16[1,128,256]{2,1,0:T(8,128)(2,1)S(1)}, u32[]{:S(2)}, u32[]{:S(2)}) collective-permute-start(bf16[1,128,256]{2,1,0:T(8,128)(2,1)S(1)} %get-tuple-element.18.keyval_refs_0__0_), channel_id=1, source_target_pairs={{0,16},{2,18},{4,20},{6,22},{8,24},{10,26},{12,28},{14,30},{16,0},... | collective-permute-start | bytes 196616 | tf_op jit(solution)/shard_map/ppermute | solution.py:99
  22.2 1.6 %collective-permute-start.2 = (bf16[16,8192]{1,0:T(8,128)(2,1)S(1)}, bf16[16,8192]{1,0:T(8,128)(2,1)S(1)}, u32[]{:S(2)}, u32[]{:S(2)}) collective-permute-start(bf16[16,8192]{1,0:T(8,128)(2,1)S(1)} %slice.22), channel_id=1, source_target_pairs={{0,1},{1,0},{2,3},{3,2},{4,5},{5,4},{6,7},{7,6},{8,9},{9,8},{10,11... | collective-permute-start | bytes 786440 | tf_op jit(solution)/shard_map/ppermute | solution.py:245
  24.8 1.6 %collective-permute-start.5 = (bf16[2,128,256]{2,1,0:T(8,128)(2,1)S(1)}, bf16[2,128,256]{2,1,0:T(8,128)(2,1)S(1)}, u32[]{:S(2)}, u32[]{:S(2)}) collective-permute-start(bf16[2,128,256]{2,1,0:T(8,128)(2,1)S(1)} %pad_maximum_fusion.5), channel_id=1, source_target_pairs={{0,4},{2,6},{4,0},{6,2},{8,12},{10,14},{12,8},{14,10},{16,20},{18,... | collective-permute-start | bytes 393224 | tf_op jit(solution)/shard_map/ppermute | solution.py:99
  26.4 1.6 %collective-permute-start = (bf16[48,2048]{1,0:T(8,128)(2,1)S(1)}, bf16[48,2048]{1,0:T(8,128)(2,1)S(1)}, u32[]{:S(2)}, u32[]{:S(2)}) collective-permute-start(bf16[48,2048]{1,0:T(8,128)(2,1)S(1)} %slice.20), channel_id=1, source_target_pairs={{0,1},{1,0},{2,3},{3,2},{4,5},{5,4},{6,7},{7,6},{8,9},{9,8},{10,11... | collective-permute-start | bytes 589832 | tf_op jit(solution)/shard_map/ppermute | solution.py:245
  28.0 1.9 %collective-permute-done.5.keyval_refs_0__2_ = bf16[2,128,256]{2,1,0:T(8,128)(2,1)S(1)} collective-permute-done((bf16[2,128,256]{2,1,0:T(8,128)(2,1)S(1)}, bf16[2,128,256]{2,1,0:T(8,128)(2,1)S(1)}, u32[]{:S(2)}, u32[]{:S(2)}) %collective-permute-start.5) | collective-permute-done | bytes 131104 | tf_op jit(solution)/shard_map/ppermute | solution.py:99
  29.9 1.6 %collective-permute-start.6 = (bf16[4,128,256]{2,1,0:T(8,128)(2,1)S(1)}, bf16[4,128,256]{2,1,0:T(8,128)(2,1)S(1)}, u32[]{:S(2)}, u32[]{:S(2)}) collective-permute-start(bf16[4,128,256]{2,1,0:T(8,128)(2,1)S(1)} %pad_maximum_fusion.2), channel_id=1, source_target_pairs={{0,8},{2,10},{4,12},{6,14},{8,0},{10,2},{12,4},{14,6},{16,24},{18,... | collective-permute-start | bytes 786440 | tf_op jit(solution)/shard_map/ppermute | solution.py:99
  31.5 16.0 %collective-permute-done.2.refs_0_ = bf16[16,8192]{1,0:T(8,128)(2,1)S(1)} collective-permute-done((bf16[16,8192]{1,0:T(8,128)(2,1)S(1)}, bf16[16,8192]{1,0:T(8,128)(2,1)S(1)}, u32[]{:S(2)}, u32[]{:S(2)}) %collective-permute-start.2) | collective-permute-done | bytes 262176 | tf_op jit(solution)/shard_map/ppermute | solution.py:245
  47.5 2.3 %shard_map.57 = (bf16[80,512]{1,0:T(8,128)(2,1)S(1)}, bf16[1,80,256]{2,1,0:T(8,128)(2,1)S(1)}) custom-call(bf16[16,8192]{1,0:T(8,128)(2,1)S(1)} %collective-permute-done.2.refs_0_, bf16[64,8192]{1,0:T(8,128)(2,1)S(1)} %collective-permute-done.3.refs_1_, bf16[8192,512]{1,0:T(8,128)(2,1)S(1)} %copy-done, bf16[8192,256]{1,0:T(8,128)(2,1)S(1)} %copy-done.1), custom_call_target="tpu_custom_call" | custom-call | flops 1006632960 | bytes 14016512 | tf_op jit(solution)/shard_map/pallas_call | solution.py:69
  49.8 3.2 %collective-permute-start.8 = (bf16[1,80,256]{2,1,0:T(8,128)(2,1)S(1)}, bf16[1,80,256]{2,1,0:T(8,128)(2,1)S(1)}, u32[]{:S(2)}, u32[]{:S(2)}) collective-permute-start(bf16[1,80,256]{2,1,0:T(8,128)(2,1)S(1)} %get-tuple-element.19.keyval_refs_1__0_), channel_id=1, source_target_pairs={{0,16},{2,18},{4,20},{6,22},{8,24},{10,26},{12,28},{14,30},{16,0},... | collective-permute-start | bytes 122888 | tf_op jit(solution)/shard_map/ppermute | solution.py:99
  53.0 2.8 %shard_map.55 = (f32[48,512]{1,0:T(8,128)S(1)}, f32[48,256]{1,0:T(8,128)S(1)}) custom-call(bf16[48,6144]{1,0:T(8,128)(2,1)} %collective-permute-done.1.refs_0_, bf16[8192,512]{1,0:T(8,128)(2,1)S(1)} %bitcast.9, bf16[8192,256]{1,0:T(8,128)(2,1)S(1)} %copy-done.1), custom_call_target="tpu_custom_call" | custom-call | flops 452984832 | bytes 10100736 | tf_op jit(solution)/shard_map/pallas_call | solution.py:69
  55.8 2.0 %shard_map.58 = (bf16[16,32,512]{2,1,0:T(8,128)(2,1)}, bf16[1,48,256]{2,1,0:T(8,128)(2,1)S(1)}) custom-call(s32[8]{0:T(128)S(1)} %pad_add_fusion.1.refs_10_.refs_0_, bf16[48,2048]{1,0:T(8,128)(2,1)S(1)} %collective-permute-done.refs_1_, bf16[8192,512]{1,0:T(8,128)(2,1)S(1)} %bitcast.9, bf16[8192,256]{1,0:T(8,128)(2,1)S(1)} %copy-done.1, ...), custom_call_target="tpu_custom_call" | custom-call | flops 150994944 | bytes 3416064 | tf_op jit(solution)/shard_map/pallas_call | solution.py:69
  57.8 3.9 %all-to-all-start = ((bf16[16,32,512]{2,1,0:T(8,128)(2,1)}), bf16[16,32,512]{2,1,0:T(8,128)(2,1)S(1)}, u32[]{:S(2)}, u32[]{:S(2)}) async-start(bf16[16,32,512]{2,1,0:T(8,128)(2,1)} %get-tuple-element.17), calls=%async_computation | async-start | bytes 1048576 | tf_op jit(solution)/shard_map/all_to_all | solution.py:315
  61.8 2.8 %collective-permute-start.12 = (bf16[1,48,256]{2,1,0:T(8,128)(2,1)S(1)}, bf16[1,48,256]{2,1,0:T(8,128)(2,1)S(1)}, u32[]{:S(2)}, u32[]{:S(2)}) collective-permute-start(bf16[1,48,256]{2,1,0:T(8,128)(2,1)S(1)} %get-tuple-element.20.keyval_refs_2__0_), channel_id=1, source_target_pairs={{0,16},{2,18},{4,20},{6,22},{8,24},{10,26},{12,28},{14,30},{16,0},... | collective-permute-start | bytes 73736 | tf_op jit(solution)/shard_map/ppermute | solution.py:99
  64.6 1.5 %collective-permute-start.9 = (bf16[2,80,256]{2,1,0:T(8,128)(2,1)S(1)}, bf16[2,80,256]{2,1,0:T(8,128)(2,1)S(1)}, u32[]{:S(2)}, u32[]{:S(2)}) collective-permute-start(bf16[2,80,256]{2,1,0:T(8,128)(2,1)S(1)} %pad_maximum_fusion.7), channel_id=1, source_target_pairs={{0,4},{2,6},{4,0},{6,2},{8,12},{10,14},{12,8},{14,10},{16,20},{18,... | collective-permute-start | bytes 245768 | tf_op jit(solution)/shard_map/ppermute | solution.py:99
  66.1 11.9 %collective-permute-done.12.keyval_refs_2__1_ = bf16[1,48,256]{2,1,0:T(8,128)(2,1)S(1)} collective-permute-done((bf16[1,48,256]{2,1,0:T(8,128)(2,1)S(1)}, bf16[1,48,256]{2,1,0:T(8,128)(2,1)S(1)}, u32[]{:S(2)}, u32[]{:S(2)}) %collective-permute-start.12) | collective-permute-done | bytes 24608 | tf_op jit(solution)/shard_map/ppermute | solution.py:99
  79.8 2.4 %collective-permute-done.13.keyval_refs_2__2_ = bf16[2,48,256]{2,1,0:T(8,128)(2,1)S(1)} collective-permute-done((bf16[2,48,256]{2,1,0:T(8,128)(2,1)S(1)}, bf16[2,48,256]{2,1,0:T(8,128)(2,1)S(1)}, u32[]{:S(2)}, u32[]{:S(2)}) %collective-permute-start.13) | collective-permute-done | bytes 49184 | tf_op jit(solution)/shard_map/ppermute | solution.py:99
  82.2 3.7 %collective-permute-done.10.keyval_refs_1__3_ = bf16[4,80,256]{2,1,0:T(8,128)(2,1)S(1)} collective-permute-done((bf16[4,80,256]{2,1,0:T(8,128)(2,1)S(1)}, bf16[4,80,256]{2,1,0:T(8,128)(2,1)S(1)}, u32[]{:S(2)}, u32[]{:S(2)}) %collective-permute-start.10) | collective-permute-done | bytes 163872 | tf_op jit(solution)/shard_map/ppermute | solution.py:99
  88.6 5.7 %attend.1 = bf16[256,512]{1,0:T(8,128)(2,1)} custom-call(s32[4]{0:T(128)S(1)} %pad_add_fusion.refs_3_.info_ref, s32[8]{0:T(128)S(1)} %select_reduce_fusion.4.refs_4_.source_ref, s32[8]{0:T(128)S(1)} %convert_reduce_fusion.refs_5_.rank_ref, s32[136]{0:T(256)S(1)} %broadcast_subtract_fusion.refs_6_.item_block_ref, ...), custom_call_target="tpu_custom_call" | custom-call | tf_op jit(solution)/shard_map/attend/pallas_call | solution.py:327
  (60 shorter events, 9.0 us)
Async XLA Ops:
  0.0 11.6 %copy-start.2 = (bf16[128,8192]{1,0:T(8,128)(2,1)S(1)}, bf16[128,8192]{1,0:T(8,128)(2,1)}, u32[]{:S(2)}) copy-start(bf16[128,8192]{1,0:T(8,128)(2,1)} %refs_0_.1) | copy-start | bytes 6291460
  2.1 50.9 %collective-permute-start.1 = (bf16[48,6144]{1,0:T(8,128)(2,1)}, bf16[48,6144]{1,0:T(8,128)(2,1)}, u32[]{:S(2)}, u32[]{:S(2)}) collective-permute-start(bf16[48,6144]{1,0:T(8,128)(2,1)} %slice.21), channel_id=1, source_target_pairs={{0,1},{1,0},{2,3},{3,2},{4,5},{5,4},{6,7},{7,6},{8,9},{9,8},{10,11... | collective-permute-start | bytes 1769480 | tf_op jit(solution)/shard_map/ppermute | solution.py:245
  7.3 40.2 %collective-permute-start.3 = (bf16[64,8192]{1,0:T(8,128)(2,1)}, bf16[64,8192]{1,0:T(8,128)(2,1)S(1)}, u32[]{:S(2)}, u32[]{:S(2)}) collective-permute-start(bf16[64,8192]{1,0:T(8,128)(2,1)} %slice.23), channel_id=1, source_target_pairs={{0,1},{1,0},{2,3},{3,2},{4,5},{5,4},{6,7},{7,6},{8,9},{9,8},{10,11... | collective-permute-start | bytes 3145736 | tf_op jit(solution)/shard_map/ppermute | solution.py:245
  11.6 3.4 %copy-start = (bf16[8192,512]{1,0:T(8,128)(2,1)S(1)}, bf16[8192,512]{1,0:T(8,128)(2,1)}, u32[]{:S(2)}) copy-start(bf16[8192,512]{1,0:T(8,128)(2,1)} %refs_2_.7) | copy-start | bytes 25165828
  15.0 2.2 %copy-start.1 = (bf16[8192,256]{1,0:T(8,128)(2,1)S(1)}, bf16[8192,256]{1,0:T(8,128)(2,1)}, u32[]{:S(2)}) copy-start(bf16[8192,256]{1,0:T(8,128)(2,1)} %refs_3_.3) | copy-start | bytes 12582916
  19.0 5.8 %collective-permute-start.4 = (bf16[1,128,256]{2,1,0:T(8,128)(2,1)S(1)}, bf16[1,128,256]{2,1,0:T(8,128)(2,1)S(1)}, u32[]{:S(2)}, u32[]{:S(2)}) collective-permute-start(bf16[1,128,256]{2,1,0:T(8,128)(2,1)S(1)} %get-tuple-element.18.keyval_refs_0__0_), channel_id=1, source_target_pairs={{0,16},{2,18},{4,20},{6,22},{8,24},{10,26},{12,28},{14,30},{16,0},... | collective-permute-start | bytes 196616 | tf_op jit(solution)/shard_map/ppermute | solution.py:99
  22.2 30.8 %slice-start = ((s8[8388608]{0:T(1024)(128)(4,1)}), s8[4194304]{0:T(1024)(128)(4,1)S(1)}, s32[]{:S(2)}) async-start(s8[8388608]{0:T(1024)(128)(4,1)} %bitcast.8), calls=%async_computation.1 | async-start | bytes 8388608
  22.2 25.3 %collective-permute-start.2 = (bf16[16,8192]{1,0:T(8,128)(2,1)S(1)}, bf16[16,8192]{1,0:T(8,128)(2,1)S(1)}, u32[]{:S(2)}, u32[]{:S(2)}) collective-permute-start(bf16[16,8192]{1,0:T(8,128)(2,1)S(1)} %slice.22), channel_id=1, source_target_pairs={{0,1},{1,0},{2,3},{3,2},{4,5},{5,4},{6,7},{7,6},{8,9},{9,8},{10,11... | collective-permute-start | bytes 786440 | tf_op jit(solution)/shard_map/ppermute | solution.py:245
  24.8 5.0 %collective-permute-start.5 = (bf16[2,128,256]{2,1,0:T(8,128)(2,1)S(1)}, bf16[2,128,256]{2,1,0:T(8,128)(2,1)S(1)}, u32[]{:S(2)}, u32[]{:S(2)}) collective-permute-start(bf16[2,128,256]{2,1,0:T(8,128)(2,1)S(1)} %pad_maximum_fusion.5), channel_id=1, source_target_pairs={{0,4},{2,6},{4,0},{6,2},{8,12},{10,14},{12,8},{14,10},{16,20},{18,... | collective-permute-start | bytes 393224 | tf_op jit(solution)/shard_map/ppermute | solution.py:99
  26.4 29.4 %collective-permute-start = (bf16[48,2048]{1,0:T(8,128)(2,1)S(1)}, bf16[48,2048]{1,0:T(8,128)(2,1)S(1)}, u32[]{:S(2)}, u32[]{:S(2)}) collective-permute-start(bf16[48,2048]{1,0:T(8,128)(2,1)S(1)} %slice.20), channel_id=1, source_target_pairs={{0,1},{1,0},{2,3},{3,2},{4,5},{5,4},{6,7},{7,6},{8,9},{9,8},{10,11... | collective-permute-start | bytes 589832 | tf_op jit(solution)/shard_map/ppermute | solution.py:245
  29.9 23.1 %slice-start.1 = ((s8[8388608]{0:T(1024)(128)(4,1)}), s8[4194304]{0:T(1024)(128)(4,1)S(1)}, s32[]{:S(2)}) async-start(s8[8388608]{0:T(1024)(128)(4,1)} %bitcast.8), calls=%async_computation.2 | async-start | bytes 8388608
  29.9 49.8 %collective-permute-start.6 = (bf16[4,128,256]{2,1,0:T(8,128)(2,1)S(1)}, bf16[4,128,256]{2,1,0:T(8,128)(2,1)S(1)}, u32[]{:S(2)}, u32[]{:S(2)}) collective-permute-start(bf16[4,128,256]{2,1,0:T(8,128)(2,1)S(1)} %pad_maximum_fusion.2), channel_id=1, source_target_pairs={{0,8},{2,10},{4,12},{6,14},{8,0},{10,2},{12,4},{14,6},{16,24},{18,... | collective-permute-start | bytes 786440 | tf_op jit(solution)/shard_map/ppermute | solution.py:99
  49.8 14.8 %collective-permute-start.8 = (bf16[1,80,256]{2,1,0:T(8,128)(2,1)S(1)}, bf16[1,80,256]{2,1,0:T(8,128)(2,1)S(1)}, u32[]{:S(2)}, u32[]{:S(2)}) collective-permute-start(bf16[1,80,256]{2,1,0:T(8,128)(2,1)S(1)} %get-tuple-element.19.keyval_refs_1__0_), channel_id=1, source_target_pairs={{0,16},{2,18},{4,20},{6,22},{8,24},{10,26},{12,28},{14,30},{16,0},... | collective-permute-start | bytes 122888 | tf_op jit(solution)/shard_map/ppermute | solution.py:99
  57.8 30.7 %all-to-all-start = ((bf16[16,32,512]{2,1,0:T(8,128)(2,1)}), bf16[16,32,512]{2,1,0:T(8,128)(2,1)S(1)}, u32[]{:S(2)}, u32[]{:S(2)}) async-start(bf16[16,32,512]{2,1,0:T(8,128)(2,1)} %get-tuple-element.17), calls=%async_computation | async-start | bytes 1048576 | tf_op jit(solution)/shard_map/all_to_all | solution.py:315
  61.8 16.3 %collective-permute-start.12 = (bf16[1,48,256]{2,1,0:T(8,128)(2,1)S(1)}, bf16[1,48,256]{2,1,0:T(8,128)(2,1)S(1)}, u32[]{:S(2)}, u32[]{:S(2)}) collective-permute-start(bf16[1,48,256]{2,1,0:T(8,128)(2,1)S(1)} %get-tuple-element.20.keyval_refs_2__0_), channel_id=1, source_target_pairs={{0,16},{2,18},{4,20},{6,22},{8,24},{10,26},{12,28},{14,30},{16,0},... | collective-permute-start | bytes 73736 | tf_op jit(solution)/shard_map/ppermute | solution.py:99
  64.6 14.9 %collective-permute-start.9 = (bf16[2,80,256]{2,1,0:T(8,128)(2,1)S(1)}, bf16[2,80,256]{2,1,0:T(8,128)(2,1)S(1)}, u32[]{:S(2)}, u32[]{:S(2)}) collective-permute-start(bf16[2,80,256]{2,1,0:T(8,128)(2,1)S(1)} %pad_maximum_fusion.7), channel_id=1, source_target_pairs={{0,4},{2,6},{4,0},{6,2},{8,12},{10,14},{12,8},{14,10},{16,20},{18,... | collective-permute-start | bytes 245768 | tf_op jit(solution)/shard_map/ppermute | solution.py:99
  78.0 4.1 %collective-permute-start.13 = (bf16[2,48,256]{2,1,0:T(8,128)(2,1)S(1)}, bf16[2,48,256]{2,1,0:T(8,128)(2,1)S(1)}, u32[]{:S(2)}, u32[]{:S(2)}) collective-permute-start(bf16[2,48,256]{2,1,0:T(8,128)(2,1)S(1)} %pad_maximum_fusion.8), channel_id=1, source_target_pairs={{0,4},{2,6},{4,0},{6,2},{8,12},{10,14},{12,8},{14,10},{16,20},{18,... | collective-permute-start | bytes 147464 | tf_op jit(solution)/shard_map/ppermute | solution.py:99
  79.5 6.4 %collective-permute-start.10 = (bf16[4,80,256]{2,1,0:T(8,128)(2,1)S(1)}, bf16[4,80,256]{2,1,0:T(8,128)(2,1)S(1)}, u32[]{:S(2)}, u32[]{:S(2)}) collective-permute-start(bf16[4,80,256]{2,1,0:T(8,128)(2,1)S(1)} %pad_maximum_fusion.4), channel_id=1, source_target_pairs={{0,8},{2,10},{4,12},{6,14},{8,0},{10,2},{12,4},{14,6},{16,24},{18,... | collective-permute-start | bytes 491528 | tf_op jit(solution)/shard_map/ppermute | solution.py:99
  79.7 7.4 %collective-permute-start.7 = (bf16[8,128,256]{2,1,0:T(8,128)(2,1)S(1)}, bf16[8,128,256]{2,1,0:T(8,128)(2,1)S(1)}, u32[]{:S(2)}, u32[]{:S(2)}) collective-permute-start(bf16[8,128,256]{2,1,0:T(8,128)(2,1)S(1)} %pad_maximum_fusion), channel_id=1, source_target_pairs={{0,2},{2,0},{4,6},{6,4},{8,10},{10,8},{12,14},{14,12},{16,18},{18,... | collective-permute-start | bytes 1572872 | tf_op jit(solution)/shard_map/ppermute | solution.py:99
  82.2 4.9 %collective-permute-start.14 = (bf16[4,48,256]{2,1,0:T(8,128)(2,1)S(1)}, bf16[4,48,256]{2,1,0:T(8,128)(2,1)S(1)}, u32[]{:S(2)}, u32[]{:S(2)}) collective-permute-start(bf16[4,48,256]{2,1,0:T(8,128)(2,1)S(1)} %pad_maximum_fusion.6), channel_id=1, source_target_pairs={{0,8},{2,10},{4,12},{6,14},{8,0},{10,2},{12,4},{14,6},{16,24},{18,... | collective-permute-start | bytes 294920 | tf_op jit(solution)/shard_map/ppermute | solution.py:99
  86.0 2.6 %collective-permute-start.11 = (bf16[8,80,256]{2,1,0:T(8,128)(2,1)S(1)}, bf16[8,80,256]{2,1,0:T(8,128)(2,1)S(1)}, u32[]{:S(2)}, u32[]{:S(2)}) collective-permute-start(bf16[8,80,256]{2,1,0:T(8,128)(2,1)S(1)} %pad_maximum_fusion.1), channel_id=1, source_target_pairs={{0,2},{2,0},{4,6},{6,4},{8,10},{10,8},{12,14},{14,12},{16,18},{18,... | collective-permute-start | bytes 983048 | tf_op jit(solution)/shard_map/ppermute | solution.py:99
  87.1 1.5 %collective-permute-start.15 = (bf16[8,48,256]{2,1,0:T(8,128)(2,1)S(1)}, bf16[8,48,256]{2,1,0:T(8,128)(2,1)S(1)}, u32[]{:S(2)}, u32[]{:S(2)}) collective-permute-start(bf16[8,48,256]{2,1,0:T(8,128)(2,1)S(1)} %pad_maximum_fusion.3), channel_id=1, source_target_pairs={{0,2},{2,0},{4,6},{6,4},{8,10},{10,8},{12,14},{14,12},{16,18},{18,... | collective-permute-start | bytes 589832 | tf_op jit(solution)/shard_map/ppermute | solution.py:99

commit v3 on v2

--- a/solution.py
+++ b/solution.py
@@ -11,7 +11,7 @@
 
 NEG_FILL = -1e30
 LOG2E = 1.4426950408889634
-UNROLL = 8
+UNROLL = 12
 
 
 def route(queries, target_ref, send_ref):
@@ -161,10 +161,11 @@
         valt_ref[tile] = value_ref[tile].T
 
     for block in range(blocks):
-        for head in range(heads):
-            query_ref[block, head * block_len : (head + 1) * block_len, :] = arrived_ref[
-                source_ref[block], :, head * dim : (head + 1) * dim
-            ]
+        heads_rows = [
+            arrived_ref[source_ref[block], :, head * dim : (head + 1) * dim]
+            for head in range(heads)
+        ]
+        query_ref[block] = jnp.concatenate(heads_rows, axis=0).T
 
     max_ref[...] = jnp.full_like(max_ref, NEG_FILL)
     sum_ref[...] = jnp.zeros_like(sum_ref)
@@ -182,7 +183,7 @@
             scores = lax.dot_general(
                 key_ref[tile],
                 query_ref[safe],
-                (((1,), (1,)), ((), ())),
+                (((1,), (0,)), ((), ())),
                 preferred_element_type=jnp.float32,
             )
             base = tile * rows
@@ -333,7 +334,7 @@
             pltpu.VMEM((count, rows, dim), jnp.bfloat16),
             pltpu.VMEM((count, rows, dim), jnp.bfloat16),
             pltpu.VMEM((count, dim, rows), jnp.bfloat16),
-            pltpu.VMEM((per, per_block, dim), jnp.bfloat16),
+            pltpu.VMEM((per, dim, per_block), jnp.bfloat16),
             pltpu.VMEM((per + 1, per_block), jnp.float32),
             pltpu.VMEM((per + 1, per_block), jnp.float32),
             pltpu.VMEM((per + 1, dim, per_block), jnp.float32),

time: 94.7 us -> 94.1 us (level)
  no operation moved by 1% of the time
where the time goes in v3:
time: 94.1 us; the launch traced here: 93.6 us
  waiting for transfers between devices  39.3 us (42%)
  starting transfers between devices  25.8 us (27%)
  Pallas kernels  13.9 us (15%)
  local copies, waits for them, and re-layouts  11.1 us (12%)
  other arithmetic  2.58 us (3%)
  between operations  0.95 us (1%)
    ppermute x12, waiting for transfers between devices, gather_all(): pieces.append(lax.ppermute(held, 'ctx', pairs))  23.3 us
    ppermute x4, waiting for transfers between devices, shifted(): lax.ppermute(part, 'tp', [(i, (i + shift) % groups) for i in range(groups)])  16 us
    ppermute x12, starting transfers between devices, gather_all(): pieces.append(lax.ppermute(held, 'ctx', pairs))  15.8 us
    pallas_call x4, Pallas kernels, project(): pl.pallas_call(functools.partial(project_kernel, len(row_parts), begin, b...  8.88 us
    ppermute x4, starting transfers between devices, shifted(): lax.ppermute(part, 'tp', [(i, (i + shift) % groups) for i in range(groups)])  6.08 us
    unnamed x10, local copies, waits for them, and re-layouts  5.58 us
    pallas_call x1, Pallas kernels, step(): pl.pallas_call(functools.partial(attend_kernel, count, heads, tuple(segme...  5.07 us
    all_to_all x1, starting transfers between devices, step(): arrived = lax.all_to_all(send, 'ctx', 0, 0, tiled=True)  3.91 us
  transfers between devices with their start and end apart: 17, of which 8 were waited for; matrix products, arithmetic and copies ran while one was open for 6% of the time, Pallas kernels for 9%

profile of v3, /device:TPU:0, one launch (start us, length us, event | category | flops | bytes accessed | tf_op | source)
XLA Modules:
  0.0 93.6 jit_solution(5345414918611221059)
XLA Ops:
  0.0 2.1 %slice.21 = bf16[48,6144]{1,0:T(8,128)(2,1)} slice(bf16[128,8192]{1,0:T(8,128)(2,1)} %refs_0_.1), slice={[80:128], [0:6144]} | slice | bytes 1179648 | tf_op jit(solution)/shard_map/slice | solution.py:299
  2.1 3.0 %collective-permute-start.1 = (bf16[48,6144]{1,0:T(8,128)(2,1)}, bf16[48,6144]{1,0:T(8,128)(2,1)}, u32[]{:S(2)}, u32[]{:S(2)}) collective-permute-start(bf16[48,6144]{1,0:T(8,128)(2,1)} %slice.21), channel_id=1, source_target_pairs={{0,1},{1,0},{2,3},{3,2},{4,5},{5,4},{6,7},{7,6},{8,9},{9,8},{10,11... | collective-permute-start | bytes 1769480 | tf_op jit(solution)/shard_map/ppermute | solution.py:246
  5.0 2.3 %slice.23 = bf16[64,8192]{1,0:T(8,128)(2,1)} slice(bf16[128,8192]{1,0:T(8,128)(2,1)} %refs_0_.1), slice={[16:80], [0:8192]} | slice | bytes 2097152 | tf_op jit(solution)/shard_map/slice | solution.py:294
  11.6 3.4 %copy-done = bf16[8192,512]{1,0:T(8,128)(2,1)S(1)} copy-done((bf16[8192,512]{1,0:T(8,128)(2,1)S(1)}, bf16[8192,512]{1,0:T(8,128)(2,1)}, u32[]{:S(2)}) %copy-start) | copy-done | bytes 8388632
  15.0 2.2 %copy-done.1 = bf16[8192,256]{1,0:T(8,128)(2,1)S(1)} copy-done((bf16[8192,256]{1,0:T(8,128)(2,1)S(1)}, bf16[8192,256]{1,0:T(8,128)(2,1)}, u32[]{:S(2)}) %copy-start.1) | copy-done | bytes 4194328
  17.2 1.8 %shard_map.56 = (bf16[128,512]{1,0:T(8,128)(2,1)S(1)}, bf16[1,128,256]{2,1,0:T(8,128)(2,1)S(1)}) custom-call(bf16[128,8192]{1,0:T(8,128)(2,1)S(1)} %copy-done.2, bf16[8192,512]{1,0:T(8,128)(2,1)S(1)} %copy-done, bf16[8192,256]{1,0:T(8,128)(2,1)S(1)} %copy-done.1, s32[4]{0:T(128)S(1)} %pad_add_fusion.refs_3_.info_ref, ...), custom_call_target="tpu_custom_call" | custom-call | flops 1610612736 | bytes 14876672 | tf_op jit(solution)/shard_map/pallas_call | solution.py:69
  19.0 3.2 %collective-permute-start.4 = (bf16[1,128,256]{2,1,0:T(8,128)(2,1)S(1)}, bf16[1,128,256]{2,1,0:T(8,128)(2,1)S(1)}, u32[]{:S(2)}, u32[]{:S(2)}) collective-permute-start(bf16[1,128,256]{2,1,0:T(8,128)(2,1)S(1)} %get-tuple-element.18.keyval_refs_0__0_), channel_id=1, source_target_pairs={{0,16},{2,18},{4,20},{6,22},{8,24},{10,26},{12,28},{14,30},{16,0},... | collective-permute-start | bytes 196616 | tf_op jit(solution)/shard_map/ppermute | solution.py:99
  22.2 1.6 %collective-permute-start.2 = (bf16[16,8192]{1,0:T(8,128)(2,1)S(1)}, bf16[16,8192]{1,0:T(8,128)(2,1)S(1)}, u32[]{:S(2)}, u32[]{:S(2)}) collective-permute-start(bf16[16,8192]{1,0:T(8,128)(2,1)S(1)} %slice.22), channel_id=1, source_target_pairs={{0,1},{1,0},{2,3},{3,2},{4,5},{5,4},{6,7},{7,6},{8,9},{9,8},{10,11... | collective-permute-start | bytes 786440 | tf_op jit(solution)/shard_map/ppermute | solution.py:246
  24.8 1.6 %collective-permute-start.5 = (bf16[2,128,256]{2,1,0:T(8,128)(2,1)S(1)}, bf16[2,128,256]{2,1,0:T(8,128)(2,1)S(1)}, u32[]{:S(2)}, u32[]{:S(2)}) collective-permute-start(bf16[2,128,256]{2,1,0:T(8,128)(2,1)S(1)} %pad_maximum_fusion.5), channel_id=1, source_target_pairs={{0,4},{2,6},{4,0},{6,2},{8,12},{10,14},{12,8},{14,10},{16,20},{18,... | collective-permute-start | bytes 393224 | tf_op jit(solution)/shard_map/ppermute | solution.py:99
  26.4 1.6 %collective-permute-start = (bf16[48,2048]{1,0:T(8,128)(2,1)S(1)}, bf16[48,2048]{1,0:T(8,128)(2,1)S(1)}, u32[]{:S(2)}, u32[]{:S(2)}) collective-permute-start(bf16[48,2048]{1,0:T(8,128)(2,1)S(1)} %slice.20), channel_id=1, source_target_pairs={{0,1},{1,0},{2,3},{3,2},{4,5},{5,4},{6,7},{7,6},{8,9},{9,8},{10,11... | collective-permute-start | bytes 589832 | tf_op jit(solution)/shard_map/ppermute | solution.py:246
  28.0 1.9 %collective-permute-done.5.keyval_refs_0__2_ = bf16[2,128,256]{2,1,0:T(8,128)(2,1)S(1)} collective-permute-done((bf16[2,128,256]{2,1,0:T(8,128)(2,1)S(1)}, bf16[2,128,256]{2,1,0:T(8,128)(2,1)S(1)}, u32[]{:S(2)}, u32[]{:S(2)}) %collective-permute-start.5) | collective-permute-done | bytes 131104 | tf_op jit(solution)/shard_map/ppermute | solution.py:99
  29.9 1.6 %collective-permute-start.6 = (bf16[4,128,256]{2,1,0:T(8,128)(2,1)S(1)}, bf16[4,128,256]{2,1,0:T(8,128)(2,1)S(1)}, u32[]{:S(2)}, u32[]{:S(2)}) collective-permute-start(bf16[4,128,256]{2,1,0:T(8,128)(2,1)S(1)} %pad_maximum_fusion.2), channel_id=1, source_target_pairs={{0,8},{2,10},{4,12},{6,14},{8,0},{10,2},{12,4},{14,6},{16,24},{18,... | collective-permute-start | bytes 786440 | tf_op jit(solution)/shard_map/ppermute | solution.py:99
  31.5 16.0 %collective-permute-done.2.refs_0_ = bf16[16,8192]{1,0:T(8,128)(2,1)S(1)} collective-permute-done((bf16[16,8192]{1,0:T(8,128)(2,1)S(1)}, bf16[16,8192]{1,0:T(8,128)(2,1)S(1)}, u32[]{:S(2)}, u32[]{:S(2)}) %collective-permute-start.2) | collective-permute-done | bytes 262176 | tf_op jit(solution)/shard_map/ppermute | solution.py:246
  47.5 2.3 %shard_map.57 = (bf16[80,512]{1,0:T(8,128)(2,1)S(1)}, bf16[1,80,256]{2,1,0:T(8,128)(2,1)S(1)}) custom-call(bf16[16,8192]{1,0:T(8,128)(2,1)S(1)} %collective-permute-done.2.refs_0_, bf16[64,8192]{1,0:T(8,128)(2,1)S(1)} %collective-permute-done.3.refs_1_, bf16[8192,512]{1,0:T(8,128)(2,1)S(1)} %copy-done, bf16[8192,256]{1,0:T(8,128)(2,1)S(1)} %copy-done.1), custom_call_target="tpu_custom_call" | custom-call | flops 1006632960 | bytes 14016512 | tf_op jit(solution)/shard_map/pallas_call | solution.py:69
  49.8 3.2 %collective-permute-start.8 = (bf16[1,80,256]{2,1,0:T(8,128)(2,1)S(1)}, bf16[1,80,256]{2,1,0:T(8,128)(2,1)S(1)}, u32[]{:S(2)}, u32[]{:S(2)}) collective-permute-start(bf16[1,80,256]{2,1,0:T(8,128)(2,1)S(1)} %get-tuple-element.19.keyval_refs_1__0_), channel_id=1, source_target_pairs={{0,16},{2,18},{4,20},{6,22},{8,24},{10,26},{12,28},{14,30},{16,0},... | collective-permute-start | bytes 122888 | tf_op jit(solution)/shard_map/ppermute | solution.py:99
  53.0 2.8 %shard_map.55 = (f32[48,512]{1,0:T(8,128)S(1)}, f32[48,256]{1,0:T(8,128)S(1)}) custom-call(bf16[48,6144]{1,0:T(8,128)(2,1)} %collective-permute-done.1.refs_0_, bf16[8192,512]{1,0:T(8,128)(2,1)S(1)} %bitcast.9, bf16[8192,256]{1,0:T(8,128)(2,1)S(1)} %copy-done.1), custom_call_target="tpu_custom_call" | custom-call | flops 452984832 | bytes 10100736 | tf_op jit(solution)/shard_map/pallas_call | solution.py:69
  55.8 2.0 %shard_map.58 = (bf16[16,32,512]{2,1,0:T(8,128)(2,1)}, bf16[1,48,256]{2,1,0:T(8,128)(2,1)S(1)}) custom-call(s32[8]{0:T(128)S(1)} %pad_add_fusion.1.refs_10_.refs_0_, bf16[48,2048]{1,0:T(8,128)(2,1)S(1)} %collective-permute-done.refs_1_, bf16[8192,512]{1,0:T(8,128)(2,1)S(1)} %bitcast.9, bf16[8192,256]{1,0:T(8,128)(2,1)S(1)} %copy-done.1, ...), custom_call_target="tpu_custom_call" | custom-call | flops 150994944 | bytes 3416064 | tf_op jit(solution)/shard_map/pallas_call | solution.py:69
  57.8 3.9 %all-to-all-start = ((bf16[16,32,512]{2,1,0:T(8,128)(2,1)}), bf16[16,32,512]{2,1,0:T(8,128)(2,1)S(1)}, u32[]{:S(2)}, u32[]{:S(2)}) async-start(bf16[16,32,512]{2,1,0:T(8,128)(2,1)} %get-tuple-element.17), calls=%async_computation | async-start | bytes 1048576 | tf_op jit(solution)/shard_map/all_to_all | solution.py:316
  61.8 2.8 %collective-permute-start.12 = (bf16[1,48,256]{2,1,0:T(8,128)(2,1)S(1)}, bf16[1,48,256]{2,1,0:T(8,128)(2,1)S(1)}, u32[]{:S(2)}, u32[]{:S(2)}) collective-permute-start(bf16[1,48,256]{2,1,0:T(8,128)(2,1)S(1)} %get-tuple-element.20.keyval_refs_2__0_), channel_id=1, source_target_pairs={{0,16},{2,18},{4,20},{6,22},{8,24},{10,26},{12,28},{14,30},{16,0},... | collective-permute-start | bytes 73736 | tf_op jit(solution)/shard_map/ppermute | solution.py:99
  64.6 1.5 %collective-permute-start.9 = (bf16[2,80,256]{2,1,0:T(8,128)(2,1)S(1)}, bf16[2,80,256]{2,1,0:T(8,128)(2,1)S(1)}, u32[]{:S(2)}, u32[]{:S(2)}) collective-permute-start(bf16[2,80,256]{2,1,0:T(8,128)(2,1)S(1)} %pad_maximum_fusion.7), channel_id=1, source_target_pairs={{0,4},{2,6},{4,0},{6,2},{8,12},{10,14},{12,8},{14,10},{16,20},{18,... | collective-permute-start | bytes 245768 | tf_op jit(solution)/shard_map/ppermute | solution.py:99
  66.1 11.9 %collective-permute-done.12.keyval_refs_2__1_ = bf16[1,48,256]{2,1,0:T(8,128)(2,1)S(1)} collective-permute-done((bf16[1,48,256]{2,1,0:T(8,128)(2,1)S(1)}, bf16[1,48,256]{2,1,0:T(8,128)(2,1)S(1)}, u32[]{:S(2)}, u32[]{:S(2)}) %collective-permute-start.12) | collective-permute-done | bytes 24608 | tf_op jit(solution)/shard_map/ppermute | solution.py:99
  79.8 2.4 %collective-permute-done.13.keyval_refs_2__2_ = bf16[2,48,256]{2,1,0:T(8,128)(2,1)S(1)} collective-permute-done((bf16[2,48,256]{2,1,0:T(8,128)(2,1)S(1)}, bf16[2,48,256]{2,1,0:T(8,128)(2,1)S(1)}, u32[]{:S(2)}, u32[]{:S(2)}) %collective-permute-start.13) | collective-permute-done | bytes 49184 | tf_op jit(solution)/shard_map/ppermute | solution.py:99
  82.2 3.7 %collective-permute-done.10.keyval_refs_1__3_ = bf16[4,80,256]{2,1,0:T(8,128)(2,1)S(1)} collective-permute-done((bf16[4,80,256]{2,1,0:T(8,128)(2,1)S(1)}, bf16[4,80,256]{2,1,0:T(8,128)(2,1)S(1)}, u32[]{:S(2)}, u32[]{:S(2)}) %collective-permute-start.10) | collective-permute-done | bytes 163872 | tf_op jit(solution)/shard_map/ppermute | solution.py:99
  88.6 5.1 %attend.1 = bf16[256,512]{1,0:T(8,128)(2,1)} custom-call(s32[4]{0:T(128)S(1)} %pad_add_fusion.refs_3_.info_ref, s32[8]{0:T(128)S(1)} %select_reduce_fusion.4.refs_4_.source_ref, s32[8]{0:T(128)S(1)} %convert_reduce_fusion.refs_5_.rank_ref, s32[140]{0:T(256)S(1)} %broadcast_subtract_fusion.refs_6_.item_block_ref, ...), custom_call_target="tpu_custom_call" | custom-call | tf_op jit(solution)/shard_map/attend/pallas_call | solution.py:328
  (60 shorter events, 9.0 us)
Async XLA Ops:
  0.0 11.6 %copy-start.2 = (bf16[128,8192]{1,0:T(8,128)(2,1)S(1)}, bf16[128,8192]{1,0:T(8,128)(2,1)}, u32[]{:S(2)}) copy-start(bf16[128,8192]{1,0:T(8,128)(2,1)} %refs_0_.1) | copy-start | bytes 6291460
  2.1 50.9 %collective-permute-start.1 = (bf16[48,6144]{1,0:T(8,128)(2,1)}, bf16[48,6144]{1,0:T(8,128)(2,1)}, u32[]{:S(2)}, u32[]{:S(2)}) collective-permute-start(bf16[48,6144]{1,0:T(8,128)(2,1)} %slice.21), channel_id=1, source_target_pairs={{0,1},{1,0},{2,3},{3,2},{4,5},{5,4},{6,7},{7,6},{8,9},{9,8},{10,11... | collective-permute-start | bytes 1769480 | tf_op jit(solution)/shard_map/ppermute | solution.py:246
  7.3 40.2 %collective-permute-start.3 = (bf16[64,8192]{1,0:T(8,128)(2,1)}, bf16[64,8192]{1,0:T(8,128)(2,1)S(1)}, u32[]{:S(2)}, u32[]{:S(2)}) collective-permute-start(bf16[64,8192]{1,0:T(8,128)(2,1)} %slice.23), channel_id=1, source_target_pairs={{0,1},{1,0},{2,3},{3,2},{4,5},{5,4},{6,7},{7,6},{8,9},{9,8},{10,11... | collective-permute-start | bytes 3145736 | tf_op jit(solution)/shard_map/ppermute | solution.py:246
  11.6 3.4 %copy-start = (bf16[8192,512]{1,0:T(8,128)(2,1)S(1)}, bf16[8192,512]{1,0:T(8,128)(2,1)}, u32[]{:S(2)}) copy-start(bf16[8192,512]{1,0:T(8,128)(2,1)} %refs_2_.7) | copy-start | bytes 25165828
  15.0 2.2 %copy-start.1 = (bf16[8192,256]{1,0:T(8,128)(2,1)S(1)}, bf16[8192,256]{1,0:T(8,128)(2,1)}, u32[]{:S(2)}) copy-start(bf16[8192,256]{1,0:T(8,128)(2,1)} %refs_3_.3) | copy-start | bytes 12582916
  19.0 5.8 %collective-permute-start.4 = (bf16[1,128,256]{2,1,0:T(8,128)(2,1)S(1)}, bf16[1,128,256]{2,1,0:T(8,128)(2,1)S(1)}, u32[]{:S(2)}, u32[]{:S(2)}) collective-permute-start(bf16[1,128,256]{2,1,0:T(8,128)(2,1)S(1)} %get-tuple-element.18.keyval_refs_0__0_), channel_id=1, source_target_pairs={{0,16},{2,18},{4,20},{6,22},{8,24},{10,26},{12,28},{14,30},{16,0},... | collective-permute-start | bytes 196616 | tf_op jit(solution)/shard_map/ppermute | solution.py:99
  22.2 30.8 %slice-start = ((s8[8388608]{0:T(1024)(128)(4,1)}), s8[4194304]{0:T(1024)(128)(4,1)S(1)}, s32[]{:S(2)}) async-start(s8[8388608]{0:T(1024)(128)(4,1)} %bitcast.8), calls=%async_computation.1 | async-start | bytes 8388608
  22.2 25.3 %collective-permute-start.2 = (bf16[16,8192]{1,0:T(8,128)(2,1)S(1)}, bf16[16,8192]{1,0:T(8,128)(2,1)S(1)}, u32[]{:S(2)}, u32[]{:S(2)}) collective-permute-start(bf16[16,8192]{1,0:T(8,128)(2,1)S(1)} %slice.22), channel_id=1, source_target_pairs={{0,1},{1,0},{2,3},{3,2},{4,5},{5,4},{6,7},{7,6},{8,9},{9,8},{10,11... | collective-permute-start | bytes 786440 | tf_op jit(solution)/shard_map/ppermute | solution.py:246
  24.8 5.0 %collective-permute-start.5 = (bf16[2,128,256]{2,1,0:T(8,128)(2,1)S(1)}, bf16[2,128,256]{2,1,0:T(8,128)(2,1)S(1)}, u32[]{:S(2)}, u32[]{:S(2)}) collective-permute-start(bf16[2,128,256]{2,1,0:T(8,128)(2,1)S(1)} %pad_maximum_fusion.5), channel_id=1, source_target_pairs={{0,4},{2,6},{4,0},{6,2},{8,12},{10,14},{12,8},{14,10},{16,20},{18,... | collective-permute-start | bytes 393224 | tf_op jit(solution)/shard_map/ppermute | solution.py:99
  26.4 29.4 %collective-permute-start = (bf16[48,2048]{1,0:T(8,128)(2,1)S(1)}, bf16[48,2048]{1,0:T(8,128)(2,1)S(1)}, u32[]{:S(2)}, u32[]{:S(2)}) collective-permute-start(bf16[48,2048]{1,0:T(8,128)(2,1)S(1)} %slice.20), channel_id=1, source_target_pairs={{0,1},{1,0},{2,3},{3,2},{4,5},{5,4},{6,7},{7,6},{8,9},{9,8},{10,11... | collective-permute-start | bytes 589832 | tf_op jit(solution)/shard_map/ppermute | solution.py:246
  29.9 23.1 %slice-start.1 = ((s8[8388608]{0:T(1024)(128)(4,1)}), s8[4194304]{0:T(1024)(128)(4,1)S(1)}, s32[]{:S(2)}) async-start(s8[8388608]{0:T(1024)(128)(4,1)} %bitcast.8), calls=%async_computation.2 | async-start | bytes 8388608
  29.9 49.7 %collective-permute-start.6 = (bf16[4,128,256]{2,1,0:T(8,128)(2,1)S(1)}, bf16[4,128,256]{2,1,0:T(8,128)(2,1)S(1)}, u32[]{:S(2)}, u32[]{:S(2)}) collective-permute-start(bf16[4,128,256]{2,1,0:T(8,128)(2,1)S(1)} %pad_maximum_fusion.2), channel_id=1, source_target_pairs={{0,8},{2,10},{4,12},{6,14},{8,0},{10,2},{12,4},{14,6},{16,24},{18,... | collective-permute-start | bytes 786440 | tf_op jit(solution)/shard_map/ppermute | solution.py:99
  49.8 14.8 %collective-permute-start.8 = (bf16[1,80,256]{2,1,0:T(8,128)(2,1)S(1)}, bf16[1,80,256]{2,1,0:T(8,128)(2,1)S(1)}, u32[]{:S(2)}, u32[]{:S(2)}) collective-permute-start(bf16[1,80,256]{2,1,0:T(8,128)(2,1)S(1)} %get-tuple-element.19.keyval_refs_1__0_), channel_id=1, source_target_pairs={{0,16},{2,18},{4,20},{6,22},{8,24},{10,26},{12,28},{14,30},{16,0},... | collective-permute-start | bytes 122888 | tf_op jit(solution)/shard_map/ppermute | solution.py:99
  57.8 30.7 %all-to-all-start = ((bf16[16,32,512]{2,1,0:T(8,128)(2,1)}), bf16[16,32,512]{2,1,0:T(8,128)(2,1)S(1)}, u32[]{:S(2)}, u32[]{:S(2)}) async-start(bf16[16,32,512]{2,1,0:T(8,128)(2,1)} %get-tuple-element.17), calls=%async_computation | async-start | bytes 1048576 | tf_op jit(solution)/shard_map/all_to_all | solution.py:316
  61.8 16.3 %collective-permute-start.12 = (bf16[1,48,256]{2,1,0:T(8,128)(2,1)S(1)}, bf16[1,48,256]{2,1,0:T(8,128)(2,1)S(1)}, u32[]{:S(2)}, u32[]{:S(2)}) collective-permute-start(bf16[1,48,256]{2,1,0:T(8,128)(2,1)S(1)} %get-tuple-element.20.keyval_refs_2__0_), channel_id=1, source_target_pairs={{0,16},{2,18},{4,20},{6,22},{8,24},{10,26},{12,28},{14,30},{16,0},... | collective-permute-start | bytes 73736 | tf_op jit(solution)/shard_map/ppermute | solution.py:99
  64.6 14.9 %collective-permute-start.9 = (bf16[2,80,256]{2,1,0:T(8,128)(2,1)S(1)}, bf16[2,80,256]{2,1,0:T(8,128)(2,1)S(1)}, u32[]{:S(2)}, u32[]{:S(2)}) collective-permute-start(bf16[2,80,256]{2,1,0:T(8,128)(2,1)S(1)} %pad_maximum_fusion.7), channel_id=1, source_target_pairs={{0,4},{2,6},{4,0},{6,2},{8,12},{10,14},{12,8},{14,10},{16,20},{18,... | collective-permute-start | bytes 245768 | tf_op jit(solution)/shard_map/ppermute | solution.py:99
  78.0 4.1 %collective-permute-start.13 = (bf16[2,48,256]{2,1,0:T(8,128)(2,1)S(1)}, bf16[2,48,256]{2,1,0:T(8,128)(2,1)S(1)}, u32[]{:S(2)}, u32[]{:S(2)}) collective-permute-start(bf16[2,48,256]{2,1,0:T(8,128)(2,1)S(1)} %pad_maximum_fusion.8), channel_id=1, source_target_pairs={{0,4},{2,6},{4,0},{6,2},{8,12},{10,14},{12,8},{14,10},{16,20},{18,... | collective-permute-start | bytes 147464 | tf_op jit(solution)/shard_map/ppermute | solution.py:99
  79.5 6.4 %collective-permute-start.10 = (bf16[4,80,256]{2,1,0:T(8,128)(2,1)S(1)}, bf16[4,80,256]{2,1,0:T(8,128)(2,1)S(1)}, u32[]{:S(2)}, u32[]{:S(2)}) collective-permute-start(bf16[4,80,256]{2,1,0:T(8,128)(2,1)S(1)} %pad_maximum_fusion.4), channel_id=1, source_target_pairs={{0,8},{2,10},{4,12},{6,14},{8,0},{10,2},{12,4},{14,6},{16,24},{18,... | collective-permute-start | bytes 491528 | tf_op jit(solution)/shard_map/ppermute | solution.py:99
  79.7 7.4 %collective-permute-start.7 = (bf16[8,128,256]{2,1,0:T(8,128)(2,1)S(1)}, bf16[8,128,256]{2,1,0:T(8,128)(2,1)S(1)}, u32[]{:S(2)}, u32[]{:S(2)}) collective-permute-start(bf16[8,128,256]{2,1,0:T(8,128)(2,1)S(1)} %pad_maximum_fusion), channel_id=1, source_target_pairs={{0,2},{2,0},{4,6},{6,4},{8,10},{10,8},{12,14},{14,12},{16,18},{18,... | collective-permute-start | bytes 1572872 | tf_op jit(solution)/shard_map/ppermute | solution.py:99
  82.2 4.9 %collective-permute-start.14 = (bf16[4,48,256]{2,1,0:T(8,128)(2,1)S(1)}, bf16[4,48,256]{2,1,0:T(8,128)(2,1)S(1)}, u32[]{:S(2)}, u32[]{:S(2)}) collective-permute-start(bf16[4,48,256]{2,1,0:T(8,128)(2,1)S(1)} %pad_maximum_fusion.6), channel_id=1, source_target_pairs={{0,8},{2,10},{4,12},{6,14},{8,0},{10,2},{12,4},{14,6},{16,24},{18,... | collective-permute-start | bytes 294920 | tf_op jit(solution)/shard_map/ppermute | solution.py:99
  86.0 2.6 %collective-permute-start.11 = (bf16[8,80,256]{2,1,0:T(8,128)(2,1)S(1)}, bf16[8,80,256]{2,1,0:T(8,128)(2,1)S(1)}, u32[]{:S(2)}, u32[]{:S(2)}) collective-permute-start(bf16[8,80,256]{2,1,0:T(8,128)(2,1)S(1)} %pad_maximum_fusion.1), channel_id=1, source_target_pairs={{0,2},{2,0},{4,6},{6,4},{8,10},{10,8},{12,14},{14,12},{16,18},{18,... | collective-permute-start | bytes 983048 | tf_op jit(solution)/shard_map/ppermute | solution.py:99
  87.1 1.5 %collective-permute-start.15 = (bf16[8,48,256]{2,1,0:T(8,128)(2,1)S(1)}, bf16[8,48,256]{2,1,0:T(8,128)(2,1)S(1)}, u32[]{:S(2)}, u32[]{:S(2)}) collective-permute-start(bf16[8,48,256]{2,1,0:T(8,128)(2,1)S(1)} %pad_maximum_fusion.3), channel_id=1, source_target_pairs={{0,2},{2,0},{4,6},{6,4},{8,10},{10,8},{12,14},{14,12},{16,18},{18,... | collective-permute-start | bytes 589832 | tf_op jit(solution)/shard_map/ppermute | solution.py:99
